TPU v7x, 512 devices: a 4x2x32 block of a 4x8x32 slice. The times are simulated.
512 devices in a mesh: groups: 2 (over y), ctx: 32 (over z), rep: 4 (over x), row: 2 (over core).
Axes of the slice: x: 4, y: 2, z: 32, core: 2. Of those that a mesh axis runs over, the one named last changes fastest.
The devices are a block of a 4x8x32 slice.
Arguments:
- queries: bfloat16 [4, 128, 64, 128], P(None, ('groups', 'ctx', 'row'), 'rep'), parts along dimension 1, may hold values from -8 to 8
- new_keys: bfloat16 [4, 128, 8, 128], P(None, ('groups', 'ctx', 'row'), 'rep'), parts along dimension 1, may hold values from -4.5 to 4.5
- step_new_values: bfloat16 [4, 128, 8, 128], P(None, ('groups', 'ctx', 'row'), 'rep'), parts along dimension 1, may hold values from -6 to 6
- context_keys: bfloat16 [8, 32768, 128], P('rep', ('groups', 'ctx')), parts along dimension 1, may hold values from -6 to 6
- context_values: bfloat16 [8, 32768, 128], P('rep', ('groups', 'ctx')), parts along dimension 1, may hold values from -6 to 6
- cluster_centroid_keys: bfloat16 [8, 256, 128], P('rep', ('groups', 'ctx')), parts along dimension 1, may hold values from -4 to 4
- cluster_mean_values: bfloat16 [8, 256, 128], P('rep', ('groups', 'ctx')), parts along dimension 1, may hold values from -6 to 6
- cluster_page_slot: int32 [8, 256], P('rep', 'groups'), parts along dimension 1, may hold values from 0 to 127, each once within a row
- picks: int32 [128, 8, 16], P(('groups', 'ctx', 'row'), 'rep'), parts along dimension 0, may hold values from 0 to 127, all different within a row
Outputs:
- attention: bfloat16 [4, 128, 64, 128], P(None, ('groups', 'ctx', 'row'), 'rep'), parts along dimension 1
There are 2 independent parts, one for each index of `groups`. A program takes and returns all parts, laid end to end along the dimension named above; each array names one. Nothing has to cross between parts.
Inputs may be any that keep to these rules, and one draw needn't show every extreme that they name: `picks`: for each row and key-value head, 16 different cluster ids. `cluster_page_slot`: for each key-value head, every cluster has its own page slot; slot p lies on context shard p // 4.
All inputs are finite; a program needn't handle non-finite values.
Results may differ from a plain program's by a relative error of at most 0.0027.
Values may be sent and summed in bfloat16 or wider, within the bound.
No kernel may reach another device: no remote copies, remote signals or barrier semaphores. Data moves between devices by JAX's collectives and lax.ppermute only.
A program may use at most 64 MiB of HBM per device.

v0:
```python
import functools
import math

import jax
import jax.numpy as jnp
from jax import lax
from jax.experimental import pallas as pl
from jax.experimental.pallas import tpu as pltpu
from jax.sharding import PartitionSpec as P


FLOOR_SCORE = -10000.0
MASKED = -(2.0**100)
NEAR = 4
RING = ("hi", "lo")
PEERS = ("hi", "row")
LANES = 128


def place():
    return lax.axis_index("hi") * NEAR + lax.axis_index("lo"), lax.axis_index("row")


def near_offsets(core):
    return (0, 1, -1, 2 - 4 * core)


def pack_pages(k_ref, v_ref, ck_ref, cv_ref, pages_ref, ck_own, cv_own, arrived):
    core = lax.axis_index("row")
    span, width = k_ref.shape[1:]
    near = ck_ref.shape[1]
    copies = [
        pltpu.make_async_copy(source.at[core], target, arrived.at[i])
        for i, (source, target) in enumerate(
            (
                (k_ref, pages_ref.at[pl.ds(0, span)]),
                (v_ref, pages_ref.at[pl.ds(span, span)]),
                (ck_ref, ck_own),
                (cv_ref, cv_own),
            )
        )
    ]
    for copy in copies:
        copy.start()
    for copy in copies[::-1]:
        copy.wait()
    coarse = jnp.concatenate(
        [ck_own[...].astype(jnp.float32), cv_own[...].astype(jnp.float32)]
        + [jnp.zeros((16 - 2 * near, width), jnp.float32)],
        axis=0,
    )
    pages_ref[2 * span :, :] = coarse.astype(pages_ref.dtype)


def head_queries(q_ref, heads, head):
    num_steps, _, num_heads, _ = q_ref.shape
    group = num_heads // heads
    rows = slice(head * group, (head + 1) * group)
    return [q_ref[s, 0, rows, :].astype(jnp.float32) for s in range(num_steps)]


def pack_ask(heads, picks_ref, slots_ref, q_ref, ask_ref):
    width = q_ref.shape[3]
    lane = lax.broadcasted_iota(jnp.int32, (8, width), 1)
    sub = lax.broadcasted_iota(jnp.int32, (8, width), 0)
    for head in range(heads):
        slot_free = jnp.ones((8, width), jnp.float32)
        cluster_used = jnp.zeros((8, width), jnp.float32)
        for i in range(picks_ref.shape[2]):
            pick = picks_ref[0, head, i]
            slot_free = jnp.where(lane == slots_ref[head, pick], 0.0, slot_free)
            cluster_used = jnp.where(lane == pick, 1.0, cluster_used)
        masks = jnp.where(sub == 0, slot_free, jnp.where(sub == 1, cluster_used, 0.0))
        message = jnp.concatenate(head_queries(q_ref, heads, head) + [masks], axis=0)
        message = message.astype(ask_ref.dtype)
        for peer in range(head, ask_ref.shape[0], heads):
            ask_ref[peer] = message


def tail(heads, q_ref, nk_ref, nv_ref, out_ref, stat_ref):
    num_steps, _, num_heads, width = q_ref.shape
    per_peer = num_steps * num_heads // heads
    scale = 1.0 / math.sqrt(width)
    step = lax.broadcasted_iota(jnp.int32, (per_peer, 1), 0) // (num_heads // heads)
    lane = lax.broadcasted_iota(jnp.int32, (per_peer, width), 1)
    for head in range(heads):
        queries = jnp.concatenate(head_queries(q_ref, heads, head), axis=0)
        scores = []
        for t in range(num_steps):
            key = nk_ref[t, 0, head : head + 1, :].astype(jnp.float32)
            scores.append(jnp.sum(queries * key, axis=1, keepdims=True) * scale)
        top = functools.reduce(
            jnp.maximum, [jnp.where(step >= t, scores[t], FLOOR_SCORE) for t in range(num_steps)]
        )
        total = jnp.zeros((per_peer, 1), jnp.float32)
        out = jnp.zeros((per_peer, width), jnp.float32)
        for t in range(num_steps):
            weight = jnp.where(step >= t, jnp.exp(jnp.minimum(scores[t] - top, 0.0)), 0.0)
            total += weight
            value = nv_ref[t, 0, head : head + 1, :].astype(jnp.float32)
            out += weight.astype(jnp.bfloat16).astype(jnp.float32) * value
        out_ref[head] = out
        stat_ref[head] = jnp.where(lane == 0, top, total)


def attend(span, near, ring, ask_ref, *rest):
    page_refs, reply_ref = rest[:NEAR], rest[NEAR]
    peers, height, width = ask_ref.shape
    per_peer = height - 8
    scale = 1.0 / math.sqrt(width)
    log_page = math.log(span // near)
    chunk_peers = LANES // per_peer
    position, core = place()
    shards = [lax.rem(position + off + ring, ring) for off in near_offsets(core)]
    page = span // near
    lane = lax.broadcasted_iota(jnp.int32, (page, width), 1)
    keys = []
    for ref, shard in zip(page_refs, shards):
        picker = jnp.concatenate(
            [jnp.where(lane == shard * near + p, MASKED, 0.0) for p in range(near)], axis=0
        ).astype(jnp.bfloat16)
        keys.append(jnp.concatenate([ref[0:span, :], picker], axis=1))
    ends = [ref[2 * span :, :].astype(jnp.float32) for ref in page_refs]
    blank = jnp.zeros((LANES - near * NEAR, width), jnp.float32)
    coarse_keys = jnp.concatenate([e[0:near] for e in ends] + [blank], axis=0)
    coarse_values = jnp.concatenate([e[near : 2 * near] for e in ends] + [blank], axis=0)
    coarse_values = coarse_values.astype(jnp.bfloat16)
    row = lax.broadcasted_iota(jnp.int32, (LANES, width), 0)
    column = lax.broadcasted_iota(jnp.int32, (LANES, width), 1)
    cluster = jnp.full((LANES, width), -1, jnp.int32)
    for b, shard in enumerate(shards):
        cluster = jnp.where(row // near == b, shard * near + row - b * near, cluster)
    picker = jnp.where(column == cluster, MASKED, 0.0)
    coarse_keys = jnp.concatenate([coarse_keys, picker], axis=1).astype(jnp.bfloat16)
    block_of = lax.broadcasted_iota(jnp.int32, (LANES, LANES), 1) // near
    lane8 = lax.broadcasted_iota(jnp.int32, (LANES, LANES), 1)
    contract_last = (((1,), (1,)), ((), ()))

    for chunk in range(peers // chunk_peers):
        asked = [ask_ref[chunk * chunk_peers + i] for i in range(chunk_peers)]
        queries = jnp.concatenate([a[:per_peer] for a in asked], axis=0)
        tails = [a[per_peer:].astype(jnp.float32) for a in asked]
        spread = lambda i: jnp.concatenate(
            [jnp.broadcast_to(t[i : i + 1], (per_peer, width)) for t in tails], axis=0
        ).astype(jnp.bfloat16)
        exact_queries = jnp.concatenate([queries, spread(0)], axis=1)
        coarse_queries = jnp.concatenate([queries, spread(1)], axis=1)
        coarse = (
            lax.dot_general(
                coarse_queries, coarse_keys, contract_last, preferred_element_type=jnp.float32
            )
            * scale
            + log_page
        )
        tops, totals, outs = [], [], []
        for b in range(NEAR):
            scores = (
                lax.dot_general(
                    exact_queries, keys[b], contract_last, preferred_element_type=jnp.float32
                )
                * scale
            )
            mine = block_of == b
            top = jnp.maximum(
                jnp.max(scores, axis=1, keepdims=True),
                jnp.max(jnp.where(mine, coarse, FLOOR_SCORE), axis=1, keepdims=True),
            )
            top = jnp.maximum(top, FLOOR_SCORE)
            weights = jnp.exp(scores - top)
            coarse_weights = jnp.where(mine, jnp.exp(jnp.where(mine, coarse - top, 0.0)), 0.0)
            totals.append(
                jnp.sum(weights, axis=1, keepdims=True)
                + jnp.sum(coarse_weights, axis=1, keepdims=True)
            )
            outs.append(
                jnp.dot(
                    weights.astype(jnp.bfloat16),
                    page_refs[b][span : 2 * span, :],
                    preferred_element_type=jnp.float32,
                )
                + jnp.dot(
                    coarse_weights.astype(jnp.bfloat16),
                    coarse_values,
                    preferred_element_type=jnp.float32,
                )
            )
            tops.append(top)
        best = functools.reduce(jnp.maximum, tops)
        factors = [jnp.exp(t - best) for t in tops]
        total = sum(f * t for f, t in zip(factors, totals))
        out = sum(f * o for f, o in zip(factors, outs))
        stats = jnp.where(lane8 == 0, best, jnp.where(lane8 == 1, total, 0.0))
        stats = jnp.transpose(stats)[0:8]
        for i in range(chunk_peers):
            peer = chunk * chunk_peers + i
            reply_ref[peer, 0:per_peer, :] = out[i * per_peer : (i + 1) * per_peer]
            shift = (LANES - i * per_peer) % LANES
            reply_ref[peer, per_peer:, :] = pltpu.roll(stats, shift, 1) if shift else stats


def merge(heads, reply_ref, tail_ref, tail_stat_ref, o_ref):
    num_steps, _, num_heads, _ = o_ref.shape
    group = num_heads // heads
    peers, height, _ = reply_ref.shape
    per_peer = height - 8
    stats = jnp.concatenate([reply_ref[p, per_peer:, :] for p in range(peers)], axis=0)
    stats = jnp.transpose(stats)[0:per_peer]
    results = []
    for head in range(heads):
        sources = range(head, peers, heads)
        tops = [stats[:, 8 * p : 8 * p + 1] for p in sources]
        totals = [stats[:, 8 * p + 1 : 8 * p + 2] for p in sources]
        tail_top = tail_stat_ref[head, :, 0:1]
        best = functools.reduce(jnp.maximum, tops, tail_top)
        factor = jnp.exp(tail_top - best)
        numer, denom = factor * tail_ref[head], factor * tail_stat_ref[head, :, 1:2]
        for p, top, total in zip(sources, tops, totals):
            factor = jnp.exp(top - best)
            numer += factor * reply_ref[p, 0:per_peer, :]
            denom += factor * total
        results.append(numer / denom)
    for s in range(num_steps):
        rows = [r[s * group : (s + 1) * group] for r in results]
        o_ref[s, 0] = jnp.concatenate(rows, axis=0).astype(o_ref.dtype)


VMEM = pl.BlockSpec(memory_space=pltpu.VMEM)
SMEM = pl.BlockSpec(memory_space=pltpu.SMEM)


def on_core(kernel, out_shape, in_specs, flops, mib, scratch=()):
    many = isinstance(out_shape, tuple)
    return pl.pallas_call(
        kernel,
        out_shape=out_shape,
        in_specs=in_specs,
        out_specs=(VMEM,) * len(out_shape) if many else VMEM,
        scratch_shapes=scratch,
        cost_estimate=pl.CostEstimate(flops=flops, bytes_accessed=2**20, transcendentals=0),
        compiler_params=pltpu.CompilerParams(vmem_limit_bytes=mib * 2**20),
    )


def per_device(ring, queries, new_keys, step_new_values, keys, values, cent_keys, cent_values, slots, picks):
    num_steps, _, num_heads, width = queries.shape
    heads, span = keys.shape[:2]
    near = cent_keys.shape[1]
    cores = lax.axis_size("row")
    peers = lax.axis_size("hi") * cores
    per_peer = num_steps * num_heads // heads
    height = per_peer + 8
    shape = jax.ShapeDtypeStruct
    pages = on_core(
        pack_pages,
        shape((2 * span + 16, width), jnp.bfloat16),
        [pl.BlockSpec(memory_space=pl.ANY)] * 4,
        2**16,
        4,
        [pltpu.VMEM((near, width), jnp.bfloat16)] * 2 + [pltpu.SemaphoreType.DMA((4,))],
    )(keys, values, cent_keys, cent_values)
    every = [(z, c) for z in range(ring) for c in range(cores)]
    shift = lambda of: [(((z + of(c)) % ring) * cores + c, z * cores + c) for z, c in every]
    fetched = [pages]
    for i in range(1, NEAR):
        pairs = shift(lambda c: near_offsets(c)[i])
        fetched.append(lax.ppermute(pages, RING + ("row",), pairs))
    ask = on_core(
        functools.partial(pack_ask, heads),
        shape((peers, height, width), jnp.bfloat16),
        [SMEM, SMEM, VMEM],
        2**16,
        4,
    )(picks, slots, queries)
    asked = lax.all_to_all(ask, PEERS, 0, 0, tiled=True)
    tail_out, tail_stat = on_core(
        functools.partial(tail, heads),
        (shape((heads, per_peer, width), jnp.float32),) * 2,
        [VMEM] * 3,
        2**22,
        4,
    )(queries, new_keys, step_new_values)
    reply = on_core(
        functools.partial(attend, span, near, ring),
        shape((peers, height, width), jnp.float32),
        [VMEM] * (1 + NEAR),
        4 * peers * per_peer * span * NEAR * width,
        20,
    )(asked, *fetched)
    reply = lax.all_to_all(reply, PEERS, 0, 0, tiled=True)
    return on_core(
        functools.partial(merge, heads), shape(queries.shape, jnp.bfloat16), [VMEM] * 3, 2**20, 8
    )(reply, tail_out, tail_stat)


def solution(mesh):
    sizes = mesh.shape
    names = [n for a in mesh.axis_names for n in (RING if a == "ctx" else (a,))]
    ring = sizes["ctx"]
    lengths = {**sizes, "hi": ring // NEAR, "lo": NEAR}
    split = jax.sharding.Mesh(mesh.devices.reshape([lengths[n] for n in names]), tuple(names))
    rows = ("groups",) + RING + ("row",)
    by_row = P(None, rows, "rep", None)
    by_page = P("rep", ("groups",) + RING, None)
    return jax.shard_map(
        functools.partial(per_device, ring),
        mesh=split,
        in_specs=(by_row,) * 3 + (by_page,) * 4 + (P("rep", "groups"), P(rows, "rep", None)),
        out_specs=by_row,
        check_vma=False,
    )
```

profile of v0, /device:TPU:97, one launch (start us, length us, event | category | flops | bytes accessed | tf_op | source)
XLA Modules:
  0.0 148.1 jit_solution(3455538601121215413)
XLA Ops:
  0.0 0.0 copy-start
  0.0 0.0 copy-start.2
  0.0 0.8 copy-done.2
  0.8 0.0 copy-start.8
  0.8 0.7 copy-done.8
  1.4 0.0 copy-start.9
  1.4 0.7 copy-done.9
  2.1 1.3 shard_map.91
  3.4 0.0 copy-start.4
  3.4 0.0 copy-start.5
  3.4 43.3 %all-to-all-start = ((bf16[16,40,128]{2,1,0:T(8,128)(2,1)}), bf16[16,40,128]{2,1,0:T(8,128)(2,1)S(1)}, u32[]{:S(2)}, u32[]{:S(2)}) async-start(bf16[16,40,128]{2,1,0:T(8,128)(2,1)} %shard_map.91), calls=%async_computation | async-start | bytes 327680 | tf_op jit(solution)/shard_map/all_to_all | solution.py:274
  46.7 0.0 copy-done
  46.7 0.0 copy-done.4
  46.7 0.0 copy-done.5
  46.7 0.0 copy-start.1
  46.7 0.9 copy-done.1
  47.7 0.4 shard_map.92.rest_0_
  48.0 2.0 %collective-permute-start = (bf16[1040,128]{1,0:T(8,128)(2,1)S(1)}, bf16[1040,128]{1,0:T(8,128)(2,1)S(1)}, u32[]{:S(2)}, u32[]{:S(2)}) collective-permute-start(bf16[1040,128]{1,0:T(8,128)(2,1)S(1)} %shard_map.92.rest_0_), channel_id=1, source_target_pairs={{8,0},{9,1},{16,8},{17,9},{24,16},{25,17},{32,24},{33,25},{40,32},... | collective-permute-start | bytes 798728 | tf_op jit(solution)/shard_map/ppermute | solution.py:266
  50.0 3.5 %collective-permute-start.1 = (bf16[1040,128]{1,0:T(8,128)(2,1)S(1)}, bf16[1040,128]{1,0:T(8,128)(2,1)S(1)}, u32[]{:S(2)}, u32[]{:S(2)}) collective-permute-start(bf16[1040,128]{1,0:T(8,128)(2,1)S(1)} %shard_map.92.rest_0_), channel_id=1, source_target_pairs={{248,0},{249,1},{0,8},{1,9},{8,16},{9,17},{16,24},{17,25},{24,32},... | collective-permute-start | bytes 798728 | tf_op jit(solution)/shard_map/ppermute | solution.py:266
  53.5 5.9 %collective-permute-start.2 = (bf16[1040,128]{1,0:T(8,128)(2,1)S(1)}, bf16[1040,128]{1,0:T(8,128)(2,1)S(1)}, u32[]{:S(2)}, u32[]{:S(2)}) collective-permute-start(bf16[1040,128]{1,0:T(8,128)(2,1)S(1)} %shard_map.92.rest_0_), channel_id=1, source_target_pairs={{16,0},{241,1},{24,8},{249,9},{32,16},{1,17},{40,24},{9,25},{48,32... | collective-permute-start | bytes 798728 | tf_op jit(solution)/shard_map/ppermute | solution.py:266
  59.5 9.5 %collective-permute-done.rest_1_ = bf16[1040,128]{1,0:T(8,128)(2,1)S(1)} collective-permute-done((bf16[1040,128]{1,0:T(8,128)(2,1)S(1)}, bf16[1040,128]{1,0:T(8,128)(2,1)S(1)}, u32[]{:S(2)}, u32[]{:S(2)}) %collective-permute-start) | collective-permute-done | bytes 266272 | tf_op jit(solution)/shard_map/ppermute | solution.py:266
  68.9 2.6 %collective-permute-done.1.rest_2_ = bf16[1040,128]{1,0:T(8,128)(2,1)S(1)} collective-permute-done((bf16[1040,128]{1,0:T(8,128)(2,1)S(1)}, bf16[1040,128]{1,0:T(8,128)(2,1)S(1)}, u32[]{:S(2)}, u32[]{:S(2)}) %collective-permute-start.1) | collective-permute-done | bytes 266272 | tf_op jit(solution)/shard_map/ppermute | solution.py:266
  71.5 6.6 %collective-permute-done.2.rest_3_ = bf16[1040,128]{1,0:T(8,128)(2,1)S(1)} collective-permute-done((bf16[1040,128]{1,0:T(8,128)(2,1)S(1)}, bf16[1040,128]{1,0:T(8,128)(2,1)S(1)}, u32[]{:S(2)}, u32[]{:S(2)}) %collective-permute-start.2) | collective-permute-done | bytes 266272 | tf_op jit(solution)/shard_map/ppermute | solution.py:266
  78.1 0.4 all-to-all-done.ask_ref
  78.5 6.5 %shard_map.93 = f32[16,40,128]{2,1,0:T(8,128)} custom-call(bf16[16,40,128]{2,1,0:T(8,128)(2,1)S(1)} %all-to-all-done.ask_ref, bf16[1040,128]{1,0:T(8,128)(2,1)S(1)} %shard_map.92.rest_0_, bf16[1040,128]{1,0:T(8,128)(2,1)S(1)} %collective-permute-done.rest_1_, bf16[1040,128]{1,0:T(8,128)(2,1)S(1)} %collective-permute-done.1.rest_2_, ...), custom_call_target="tpu_custom_call" | custom-call | flops 536870912 | bytes 1048576 | tf_op jit(solution)/shard_map/pallas_call | solution.py:282
  84.9 0.0 copy-start.3
  84.9 0.0 copy-start.6
  84.9 0.0 copy-start.7
  84.9 16.2 %all-to-all-start.1 = ((f32[16,40,128]{2,1,0:T(8,128)}), f32[16,40,128]{2,1,0:T(8,128)S(1)}, u32[]{:S(2)}, u32[]{:S(2)}) async-start(f32[16,40,128]{2,1,0:T(8,128)} %shard_map.93), calls=%async_computation.1 | async-start | bytes 655360 | tf_op jit(solution)/shard_map/all_to_all | solution.py:289
  101.1 0.0 copy-done.3
  101.1 0.0 copy-done.6
  101.1 0.0 copy-done.7
  101.2 0.1 shard_map.94
  101.3 45.6 %all-to-all-done.1.reply_ref = f32[16,40,128]{2,1,0:T(8,128)S(1)} async-done(((f32[16,40,128]{2,1,0:T(8,128)}), f32[16,40,128]{2,1,0:T(8,128)S(1)}, u32[]{:S(2)}, u32[]{:S(2)}) %all-to-all-start.1) | async-done | bytes 327712 | tf_op jit(solution)/shard_map/all_to_all | solution.py:289
  146.9 1.3 shard_map.95
Async XLA Ops:
  0.0 46.7 %copy-start = (bf16[2,512,128]{2,1,0:T(8,128)(2,1)S(1)}, bf16[2,512,128]{2,1,0:T(8,128)(2,1)}, u32[]{:S(2)}) copy-start(bf16[2,512,128]{2,1,0:T(8,128)(2,1)} %k_ref.1) | copy-start | bytes 786436
  0.0 0.8 copy-start.2
  0.8 0.7 copy-start.8
  1.4 0.7 copy-start.9
  3.4 43.3 %copy-start.4 = (bf16[2,4,128]{2,1,0:T(4,128)(2,1)S(1)}, bf16[2,4,128]{2,1,0:T(4,128)(2,1)}, u32[]{:S(2)}) copy-start(bf16[2,4,128]{2,1,0:T(4,128)(2,1)} %ck_ref.1) | copy-start | bytes 6148
  3.4 43.3 %copy-start.5 = (bf16[2,4,128]{2,1,0:T(4,128)(2,1)S(1)}, bf16[2,4,128]{2,1,0:T(4,128)(2,1)}, u32[]{:S(2)}) copy-start(bf16[2,4,128]{2,1,0:T(4,128)(2,1)} %cv_ref.1) | copy-start | bytes 6148
  3.4 75.1 %all-to-all-start = ((bf16[16,40,128]{2,1,0:T(8,128)(2,1)}), bf16[16,40,128]{2,1,0:T(8,128)(2,1)S(1)}, u32[]{:S(2)}, u32[]{:S(2)}) async-start(bf16[16,40,128]{2,1,0:T(8,128)(2,1)} %shard_map.91), calls=%async_computation | async-start | bytes 327680 | tf_op jit(solution)/shard_map/all_to_all | solution.py:274
  46.7 1.0 copy-start.1
  48.0 20.9 %collective-permute-start = (bf16[1040,128]{1,0:T(8,128)(2,1)S(1)}, bf16[1040,128]{1,0:T(8,128)(2,1)S(1)}, u32[]{:S(2)}, u32[]{:S(2)}) collective-permute-start(bf16[1040,128]{1,0:T(8,128)(2,1)S(1)} %shard_map.92.rest_0_), channel_id=1, source_target_pairs={{8,0},{9,1},{16,8},{17,9},{24,16},{25,17},{32,24},{33,25},{40,32},... | collective-permute-start | bytes 798728 | tf_op jit(solution)/shard_map/ppermute | solution.py:266
  50.0 21.5 %collective-permute-start.1 = (bf16[1040,128]{1,0:T(8,128)(2,1)S(1)}, bf16[1040,128]{1,0:T(8,128)(2,1)S(1)}, u32[]{:S(2)}, u32[]{:S(2)}) collective-permute-start(bf16[1040,128]{1,0:T(8,128)(2,1)S(1)} %shard_map.92.rest_0_), channel_id=1, source_target_pairs={{248,0},{249,1},{0,8},{1,9},{8,16},{9,17},{16,24},{17,25},{24,32},... | collective-permute-start | bytes 798728 | tf_op jit(solution)/shard_map/ppermute | solution.py:266
  53.5 24.5 %collective-permute-start.2 = (bf16[1040,128]{1,0:T(8,128)(2,1)S(1)}, bf16[1040,128]{1,0:T(8,128)(2,1)S(1)}, u32[]{:S(2)}, u32[]{:S(2)}) collective-permute-start(bf16[1040,128]{1,0:T(8,128)(2,1)S(1)} %shard_map.92.rest_0_), channel_id=1, source_target_pairs={{16,0},{241,1},{24,8},{249,9},{32,16},{1,17},{40,24},{9,25},{48,32... | collective-permute-start | bytes 798728 | tf_op jit(solution)/shard_map/ppermute | solution.py:266
  84.9 16.2 %copy-start.3 = (bf16[4,1,16,128]{3,2,1,0:T(8,128)(2,1)S(1)}, bf16[4,1,16,128]{3,2,1,0:T(8,128)(2,1)}, u32[]{:S(2)}) copy-start(bf16[4,1,16,128]{3,2,1,0:T(8,128)(2,1)} %q_ref.3) | copy-start | bytes 49156
  84.9 16.2 %copy-start.6 = (bf16[4,1,2,128]{3,2,1,0:T(2,128)(2,1)S(1)}, bf16[4,1,2,128]{3,2,1,0:T(2,128)(2,1)}, u32[]{:S(2)}) copy-start(bf16[4,1,2,128]{3,2,1,0:T(2,128)(2,1)} %nk_ref.1) | copy-start | bytes 6148
  84.9 16.2 %copy-start.7 = (bf16[4,1,2,128]{3,2,1,0:T(2,128)(2,1)S(1)}, bf16[4,1,2,128]{3,2,1,0:T(2,128)(2,1)}, u32[]{:S(2)}) copy-start(bf16[4,1,2,128]{3,2,1,0:T(2,128)(2,1)} %nv_ref.1) | copy-start | bytes 6148
  84.9 61.9 %all-to-all-start.1 = ((f32[16,40,128]{2,1,0:T(8,128)}), f32[16,40,128]{2,1,0:T(8,128)S(1)}, u32[]{:S(2)}, u32[]{:S(2)}) async-start(f32[16,40,128]{2,1,0:T(8,128)} %shard_map.93), calls=%async_computation.1 | async-start | bytes 655360 | tf_op jit(solution)/shard_map/all_to_all | solution.py:289
where the time goes:
time: 149 us; the launch traced here: 148 us
  starting transfers between devices  70.9 us (48%)
  waiting for transfers between devices  64.6 us (43%)
  Pallas kernels  9.5 us (6%)
  local copies, waits for them, and re-layouts  3.08 us (2%)
    all_to_all x1, waiting for transfers between devices, per_device(): reply = lax.all_to_all(reply, PEERS, 0, 0, tiled=True)  45.6 us
    all_to_all x1, starting transfers between devices, per_device(): asked = lax.all_to_all(ask, PEERS, 0, 0, tiled=True)  43.3 us
    ppermute x3, waiting for transfers between devices, per_device(): fetched.append(lax.ppermute(pages, RING + ('row',), pairs))  18.6 us
    all_to_all x1, starting transfers between devices, per_device(): reply = lax.all_to_all(reply, PEERS, 0, 0, tiled=True)  16.2 us
    ppermute x3, starting transfers between devices, per_device(): fetched.append(lax.ppermute(pages, RING + ('row',), pairs))  11.4 us
    pallas_call x1, Pallas kernels, per_device(): on_core(functools.partial(attend, span, near, ring), shape((peers, height...  6.46 us
    unnamed x20, local copies, waits for them, and re-layouts  3.08 us
  transfers between devices with their start and end apart: 5, of which 5 were waited for; matrix products, arithmetic and copies ran while one was open for 0% of the time, Pallas kernels for 0%

commit v1 on v0

--- a/solution.py
+++ b/solution.py
@@ -15,6 +15,12 @@
 RING = ("hi", "lo")
 PEERS = ("hi", "row")
 LANES = 128
+SMALLEST = 2.0**-100
+LOW_SCALE = 1024.0
+
+
+def as_bf16(x):
+    return x.astype(jnp.bfloat16).astype(jnp.float32)
 
 
 def place():
@@ -23,33 +29,6 @@
 
 def near_offsets(core):
     return (0, 1, -1, 2 - 4 * core)
-
-
-def pack_pages(k_ref, v_ref, ck_ref, cv_ref, pages_ref, ck_own, cv_own, arrived):
-    core = lax.axis_index("row")
-    span, width = k_ref.shape[1:]
-    near = ck_ref.shape[1]
-    copies = [
-        pltpu.make_async_copy(source.at[core], target, arrived.at[i])
-        for i, (source, target) in enumerate(
-            (
-                (k_ref, pages_ref.at[pl.ds(0, span)]),
-                (v_ref, pages_ref.at[pl.ds(span, span)]),
-                (ck_ref, ck_own),
-                (cv_ref, cv_own),
-            )
-        )
-    ]
-    for copy in copies:
-        copy.start()
-    for copy in copies[::-1]:
-        copy.wait()
-    coarse = jnp.concatenate(
-        [ck_own[...].astype(jnp.float32), cv_own[...].astype(jnp.float32)]
-        + [jnp.zeros((16 - 2 * near, width), jnp.float32)],
-        axis=0,
-    )
-    pages_ref[2 * span :, :] = coarse.astype(pages_ref.dtype)
 
 
 def head_queries(q_ref, heads, head):
@@ -59,10 +38,26 @@
     return [q_ref[s, 0, rows, :].astype(jnp.float32) for s in range(num_steps)]
 
 
-def pack_ask(heads, picks_ref, slots_ref, q_ref, ask_ref):
-    width = q_ref.shape[3]
+def prepare(
+    heads, picks_ref, slots_ref, q_hbm, k_ref, v_ref, ck_ref, cv_ref, pages_ref, ask_ref,
+    q_ref, ck_own, cv_own, arrived,
+):
+    core = lax.axis_index("row")
+    span, width = k_ref.shape[1:]
+    near = ck_ref.shape[1]
+    moves = (
+        (q_hbm, q_ref),
+        (ck_ref.at[core], ck_own),
+        (cv_ref.at[core], cv_own),
+        (k_ref.at[core], pages_ref.at[pl.ds(0, span)]),
+        (v_ref.at[core], pages_ref.at[pl.ds(span, span)]),
+    )
+    copies = [pltpu.make_async_copy(*move, arrived.at[i]) for i, move in enumerate(moves)]
+    for copy in copies:
+        copy.start()
     lane = lax.broadcasted_iota(jnp.int32, (8, width), 1)
     sub = lax.broadcasted_iota(jnp.int32, (8, width), 0)
+    masks = []
     for head in range(heads):
         slot_free = jnp.ones((8, width), jnp.float32)
         cluster_used = jnp.zeros((8, width), jnp.float32)
@@ -70,11 +65,23 @@
             pick = picks_ref[0, head, i]
             slot_free = jnp.where(lane == slots_ref[head, pick], 0.0, slot_free)
             cluster_used = jnp.where(lane == pick, 1.0, cluster_used)
-        masks = jnp.where(sub == 0, slot_free, jnp.where(sub == 1, cluster_used, 0.0))
-        message = jnp.concatenate(head_queries(q_ref, heads, head) + [masks], axis=0)
+        masks.append(jnp.where(sub == 0, slot_free, jnp.where(sub == 1, cluster_used, 0.0)))
+    copies[0].wait()
+    for head in range(heads):
+        message = jnp.concatenate(head_queries(q_ref, heads, head) + [masks[head]], axis=0)
         message = message.astype(ask_ref.dtype)
         for peer in range(head, ask_ref.shape[0], heads):
             ask_ref[peer] = message
+    for copy in copies[1:3]:
+        copy.wait()
+    coarse = jnp.concatenate(
+        [ck_own[...].astype(jnp.float32), cv_own[...].astype(jnp.float32)]
+        + [jnp.zeros((16 - 2 * near, width), jnp.float32)],
+        axis=0,
+    )
+    pages_ref[2 * span :, :] = coarse.astype(pages_ref.dtype)
+    for copy in copies[3:]:
+        copy.wait()
 
 
 def tail(heads, q_ref, nk_ref, nv_ref, out_ref, stat_ref):
@@ -189,13 +196,29 @@
         factors = [jnp.exp(t - best) for t in tops]
         total = sum(f * t for f, t in zip(factors, totals))
         out = sum(f * o for f, o in zip(factors, outs))
-        stats = jnp.where(lane8 == 0, best, jnp.where(lane8 == 1, total, 0.0))
+        level = jnp.where(total > 0.0, best + jnp.log(total), 2 * FLOOR_SCORE)
+        out = out * jnp.where(total > 0.0, 1.0 / total, 0.0)
+        largest = jnp.max(jnp.abs(out), axis=1, keepdims=True)
+        power = jnp.ceil(jnp.log2(jnp.maximum(largest, SMALLEST)))
+        out = out * jnp.exp2(-power)
+        high = as_bf16(level)
+        middle = as_bf16(level - high)
+        low = (level - high - middle) * LOW_SCALE
+        stats = jnp.zeros((LANES, LANES), jnp.float32)
+        for i, part in enumerate((high, middle, low, power)):
+            stats = jnp.where(lane8 == i, part, stats)
         stats = jnp.transpose(stats)[0:8]
+        turns = [pltpu.roll(stats, i * per_peer, 1) if i else stats for i in range(chunk_peers)]
+        part_of = lax.broadcasted_iota(jnp.int32, (8, LANES), 1) // per_peer
+        first_row = lax.broadcasted_iota(jnp.int32, (8, LANES), 0) == 0
         for i in range(chunk_peers):
             peer = chunk * chunk_peers + i
             reply_ref[peer, 0:per_peer, :] = out[i * per_peer : (i + 1) * per_peer]
-            shift = (LANES - i * per_peer) % LANES
-            reply_ref[peer, per_peer:, :] = pltpu.roll(stats, shift, 1) if shift else stats
+            line = jnp.zeros((8, LANES), jnp.float32)
+            for part in range(chunk_peers):
+                turned = turns[(part - i) % chunk_peers][part : part + 1]
+                line = jnp.where((part_of == part) & first_row, turned, line)
+            reply_ref[peer, per_peer:, :] = line
 
 
 def merge(heads, reply_ref, tail_ref, tail_stat_ref, o_ref):
@@ -203,21 +226,25 @@
     group = num_heads // heads
     peers, height, _ = reply_ref.shape
     per_peer = height - 8
-    stats = jnp.concatenate([reply_ref[p, per_peer:, :] for p in range(peers)], axis=0)
-    stats = jnp.transpose(stats)[0:per_peer]
+    stats = [reply_ref[p, per_peer : per_peer + 1, :] for p in range(peers)]
+    stats = jnp.transpose(
+        jnp.concatenate(stats + [jnp.zeros((LANES - peers, LANES), jnp.float32)], axis=0)
+    )
+    high, middle, low, power = (stats[i * per_peer : (i + 1) * per_peer] for i in range(4))
+    levels = high + (middle + low * (1.0 / LOW_SCALE))
+    powers = jnp.exp2(power)
     results = []
     for head in range(heads):
         sources = range(head, peers, heads)
-        tops = [stats[:, 8 * p : 8 * p + 1] for p in sources]
-        totals = [stats[:, 8 * p + 1 : 8 * p + 2] for p in sources]
+        tops = [levels[:, p : p + 1] for p in sources]
         tail_top = tail_stat_ref[head, :, 0:1]
         best = functools.reduce(jnp.maximum, tops, tail_top)
         factor = jnp.exp(tail_top - best)
         numer, denom = factor * tail_ref[head], factor * tail_stat_ref[head, :, 1:2]
-        for p, top, total in zip(sources, tops, totals):
+        for p, top in zip(sources, tops):
             factor = jnp.exp(top - best)
-            numer += factor * reply_ref[p, 0:per_peer, :]
-            denom += factor * total
+            numer += (factor * powers[:, p : p + 1]) * reply_ref[p, 0:per_peer, :]
+            denom += factor
         results.append(numer / denom)
     for s in range(num_steps):
         rows = [r[s * group : (s + 1) * group] for r in results]
@@ -226,6 +253,7 @@
 
 VMEM = pl.BlockSpec(memory_space=pltpu.VMEM)
 SMEM = pl.BlockSpec(memory_space=pltpu.SMEM)
+HBM = pl.BlockSpec(memory_space=pltpu.HBM)
 
 
 def on_core(kernel, out_shape, in_specs, flops, mib, scratch=()):
@@ -250,27 +278,25 @@
     per_peer = num_steps * num_heads // heads
     height = per_peer + 8
     shape = jax.ShapeDtypeStruct
-    pages = on_core(
-        pack_pages,
-        shape((2 * span + 16, width), jnp.bfloat16),
-        [pl.BlockSpec(memory_space=pl.ANY)] * 4,
+    pages, ask = on_core(
+        functools.partial(prepare, heads),
+        (
+            shape((2 * span + 16, width), jnp.bfloat16),
+            shape((peers, height, width), jnp.bfloat16),
+        ),
+        [SMEM] * 2 + [HBM] * 5,
         2**16,
-        4,
-        [pltpu.VMEM((near, width), jnp.bfloat16)] * 2 + [pltpu.SemaphoreType.DMA((4,))],
-    )(keys, values, cent_keys, cent_values)
+        60,
+        [pltpu.VMEM(queries.shape, jnp.bfloat16)]
+        + [pltpu.VMEM((near, width), jnp.bfloat16)] * 2
+        + [pltpu.SemaphoreType.DMA((5,))],
+    )(picks, slots, queries, keys, values, cent_keys, cent_values)
     every = [(z, c) for z in range(ring) for c in range(cores)]
     shift = lambda of: [(((z + of(c)) % ring) * cores + c, z * cores + c) for z, c in every]
     fetched = [pages]
     for i in range(1, NEAR):
         pairs = shift(lambda c: near_offsets(c)[i])
         fetched.append(lax.ppermute(pages, RING + ("row",), pairs))
-    ask = on_core(
-        functools.partial(pack_ask, heads),
-        shape((peers, height, width), jnp.bfloat16),
-        [SMEM, SMEM, VMEM],
-        2**16,
-        4,
-    )(picks, slots, queries)
     asked = lax.all_to_all(ask, PEERS, 0, 0, tiled=True)
     tail_out, tail_stat = on_core(
         functools.partial(tail, heads),
@@ -286,7 +312,8 @@
         4 * peers * per_peer * span * NEAR * width,
         20,
     )(asked, *fetched)
-    reply = lax.all_to_all(reply, PEERS, 0, 0, tiled=True)
+    reply = lax.all_to_all(reply.astype(jnp.float16), PEERS, 0, 0, tiled=True)
+    reply = reply.astype(jnp.float32)
     return on_core(
         functools.partial(merge, heads), shape(queries.shape, jnp.bfloat16), [VMEM] * 3, 2**20, 8
     )(reply, tail_out, tail_stat)

time: 149 us -> 137 us (0.919)
  the two profiles are of different devices: /device:TPU:97 before, /device:TPU:33 now
where the time goes in v1:
time: 137 us
  starting transfers between devices  71.6 us (52%)
  waiting for transfers between devices  54.2 us (40%)
  Pallas kernels  10.1 us (7%)
    all_to_all x1, starting transfers between devices, per_device(): asked = lax.all_to_all(ask, PEERS, 0, 0, tiled=True)  45 us
    all_to_all x1, waiting for transfers between devices, per_device(): reply = lax.all_to_all(reply.astype(jnp.float16), PEERS, 0, 0, tiled=True)  31.7 us
    ppermute x3, waiting for transfers between devices, per_device(): fetched.append(lax.ppermute(pages, RING + ('row',), pairs))  18.1 us
    all_to_all x1, starting transfers between devices, per_device(): reply = lax.all_to_all(reply.astype(jnp.float16), PEERS, 0, 0, tiled=True)  14.2 us
    ppermute x3, starting transfers between devices, per_device(): fetched.append(lax.ppermute(pages, RING + ('row',), pairs))  12.4 us
    pallas_call x1, Pallas kernels, per_device(): on_core(functools.partial(attend, span, near, ring), shape((peers, height...  6.16 us
    all_to_all x1, waiting for transfers between devices, per_device(): asked = lax.all_to_all(ask, PEERS, 0, 0, tiled=True)  4.36 us
  transfers between devices with their start and end apart: 5, of which 5 were waited for; matrix products, arithmetic and copies ran while one was open for 0% of the time, Pallas kernels for 0%

profile of v1, /device:TPU:33, one launch (start us, length us, event | category | flops | bytes accessed | tf_op | source)
XLA Modules:
  0.0 136.7 jit_solution(6163238607987664282)
XLA Ops:
  0.0 2.5 %shard_map.91 = (bf16[1040,128]{1,0:T(8,128)(2,1)}, bf16[16,40,128]{2,1,0:T(8,128)(2,1)}) custom-call(s32[1,2,16]{2,1,0:T(2,128)} %picks_ref.1, s32[2,128]{1,0:T(2,128)} %slots_ref.1, bf16[4,1,16,128]{3,2,1,0:T(8,128)(2,1)} %q_ref.1, bf16[2,512,128]{2,1,0:T(8,128)(2,1)} %k_ref.1, bf16[2,512,128]{2,1,0:T(8,128)(2,1)} %v_ref.1, bf16[2,4,128]{2,1,0:T(4,128)(2,1)} %ck_ref.1, ...), custom_call_target="tpu_custom_call" | custom-call | flops 65536 | bytes 1048576 | tf_op jit(solution)/shard_map/pallas_call | solution.py:281
  2.5 0.0 copy-start.3
  2.5 45.0 %all-to-all-start = ((bf16[16,40,128]{2,1,0:T(8,128)(2,1)}), bf16[16,40,128]{2,1,0:T(8,128)(2,1)S(1)}, u32[]{:S(2)}, u32[]{:S(2)}) async-start(bf16[16,40,128]{2,1,0:T(8,128)(2,1)} %get-tuple-element.9), calls=%async_computation | async-start | bytes 327680 | tf_op jit(solution)/shard_map/all_to_all | solution.py:300
  47.6 0.0 copy-done.3
  47.6 8.4 %collective-permute-start = (bf16[1040,128]{1,0:T(8,128)(2,1)S(1)}, bf16[1040,128]{1,0:T(8,128)(2,1)S(1)}, u32[]{:S(2)}, u32[]{:S(2)}) collective-permute-start(bf16[1040,128]{1,0:T(8,128)(2,1)S(1)} %copy-done.3), channel_id=1, source_target_pairs={{8,0},{9,1},{16,8},{17,9},{24,16},{25,17},{32,24},{33,25},{40,32},... | collective-permute-start | bytes 798728 | tf_op jit(solution)/shard_map/ppermute | solution.py:299
  56.0 2.0 %collective-permute-start.1 = (bf16[1040,128]{1,0:T(8,128)(2,1)S(1)}, bf16[1040,128]{1,0:T(8,128)(2,1)S(1)}, u32[]{:S(2)}, u32[]{:S(2)}) collective-permute-start(bf16[1040,128]{1,0:T(8,128)(2,1)S(1)} %copy-done.3), channel_id=1, source_target_pairs={{248,0},{249,1},{0,8},{1,9},{8,16},{9,17},{16,24},{17,25},{24,32},... | collective-permute-start | bytes 798728 | tf_op jit(solution)/shard_map/ppermute | solution.py:299
  58.0 2.0 %collective-permute-start.2 = (bf16[1040,128]{1,0:T(8,128)(2,1)S(1)}, bf16[1040,128]{1,0:T(8,128)(2,1)S(1)}, u32[]{:S(2)}, u32[]{:S(2)}) collective-permute-start(bf16[1040,128]{1,0:T(8,128)(2,1)S(1)} %copy-done.3), channel_id=1, source_target_pairs={{16,0},{241,1},{24,8},{249,9},{32,16},{1,17},{40,24},{9,25},{48,32... | collective-permute-start | bytes 798728 | tf_op jit(solution)/shard_map/ppermute | solution.py:299
  59.9 9.9 %collective-permute-done.rest_1_ = bf16[1040,128]{1,0:T(8,128)(2,1)S(1)} collective-permute-done((bf16[1040,128]{1,0:T(8,128)(2,1)S(1)}, bf16[1040,128]{1,0:T(8,128)(2,1)S(1)}, u32[]{:S(2)}, u32[]{:S(2)}) %collective-permute-start) | collective-permute-done | bytes 266272 | tf_op jit(solution)/shard_map/ppermute | solution.py:299
  69.8 5.2 %collective-permute-done.1.rest_2_ = bf16[1040,128]{1,0:T(8,128)(2,1)S(1)} collective-permute-done((bf16[1040,128]{1,0:T(8,128)(2,1)S(1)}, bf16[1040,128]{1,0:T(8,128)(2,1)S(1)}, u32[]{:S(2)}, u32[]{:S(2)}) %collective-permute-start.1) | collective-permute-done | bytes 266272 | tf_op jit(solution)/shard_map/ppermute | solution.py:299
  75.0 3.1 %collective-permute-done.2.rest_3_ = bf16[1040,128]{1,0:T(8,128)(2,1)S(1)} collective-permute-done((bf16[1040,128]{1,0:T(8,128)(2,1)S(1)}, bf16[1040,128]{1,0:T(8,128)(2,1)S(1)}, u32[]{:S(2)}, u32[]{:S(2)}) %collective-permute-start.2) | collective-permute-done | bytes 266272 | tf_op jit(solution)/shard_map/ppermute | solution.py:299
  78.1 4.4 %all-to-all-done.ask_ref = bf16[16,40,128]{2,1,0:T(8,128)(2,1)S(1)} async-done(((bf16[16,40,128]{2,1,0:T(8,128)(2,1)}), bf16[16,40,128]{2,1,0:T(8,128)(2,1)S(1)}, u32[]{:S(2)}, u32[]{:S(2)}) %all-to-all-start) | async-done | bytes 163872 | tf_op jit(solution)/shard_map/all_to_all | solution.py:300
  82.4 6.2 %shard_map.92 = f32[16,40,128]{2,1,0:T(8,128)S(1)} custom-call(bf16[16,40,128]{2,1,0:T(8,128)(2,1)S(1)} %all-to-all-done.ask_ref, bf16[1040,128]{1,0:T(8,128)(2,1)S(1)} %copy-done.3, bf16[1040,128]{1,0:T(8,128)(2,1)S(1)} %collective-permute-done.rest_1_, bf16[1040,128]{1,0:T(8,128)(2,1)S(1)} %collective-permute-done.1.rest_2_, ...), custom_call_target="tpu_custom_call" | custom-call | flops 536870912 | bytes 1048576 | tf_op jit(solution)/shard_map/pallas_call | solution.py:308
  88.6 0.7 convert_element_type.6
  89.3 0.0 copy-start
  89.3 0.0 copy-start.1
  89.3 0.0 copy-start.2
  89.3 14.2 %all-to-all-start.1 = ((f16[16,40,128]{2,1,0:T(8,128)(2,1)}), f16[16,40,128]{2,1,0:T(8,128)(2,1)S(1)}, u32[]{:S(2)}, u32[]{:S(2)}) async-start(f16[16,40,128]{2,1,0:T(8,128)(2,1)} %convert_element_type.6), calls=%async_computation.1 | async-start | bytes 327680 | tf_op jit(solution)/shard_map/all_to_all | solution.py:315
  103.5 0.0 copy-done
  103.5 0.0 copy-done.1
  103.5 0.0 copy-done.2
  103.5 0.1 shard_map.93
  103.7 31.7 %all-to-all-done.1 = f16[16,40,128]{2,1,0:T(8,128)(2,1)S(1)} async-done(((f16[16,40,128]{2,1,0:T(8,128)(2,1)}), f16[16,40,128]{2,1,0:T(8,128)(2,1)S(1)}, u32[]{:S(2)}, u32[]{:S(2)}) %all-to-all-start.1) | async-done | bytes 163872 | tf_op jit(solution)/shard_map/all_to_all | solution.py:315
  135.4 1.3 shard_map.94
  (1 shorter events, 0.0 us)
Async XLA Ops:
  2.5 45.0 %copy-start.3 = (bf16[1040,128]{1,0:T(8,128)(2,1)S(1)}, bf16[1040,128]{1,0:T(8,128)(2,1)}, u32[]{:S(2)}) copy-start(bf16[1040,128]{1,0:T(8,128)(2,1)} %get-tuple-element.10.rest_0_) | copy-start | bytes 798724
  2.5 79.9 %all-to-all-start = ((bf16[16,40,128]{2,1,0:T(8,128)(2,1)}), bf16[16,40,128]{2,1,0:T(8,128)(2,1)S(1)}, u32[]{:S(2)}, u32[]{:S(2)}) async-start(bf16[16,40,128]{2,1,0:T(8,128)(2,1)} %get-tuple-element.9), calls=%async_computation | async-start | bytes 327680 | tf_op jit(solution)/shard_map/all_to_all | solution.py:300
  47.6 22.3 %collective-permute-start = (bf16[1040,128]{1,0:T(8,128)(2,1)S(1)}, bf16[1040,128]{1,0:T(8,128)(2,1)S(1)}, u32[]{:S(2)}, u32[]{:S(2)}) collective-permute-start(bf16[1040,128]{1,0:T(8,128)(2,1)S(1)} %copy-done.3), channel_id=1, source_target_pairs={{8,0},{9,1},{16,8},{17,9},{24,16},{25,17},{32,24},{33,25},{40,32},... | collective-permute-start | bytes 798728 | tf_op jit(solution)/shard_map/ppermute | solution.py:299
  56.0 19.0 %collective-permute-start.1 = (bf16[1040,128]{1,0:T(8,128)(2,1)S(1)}, bf16[1040,128]{1,0:T(8,128)(2,1)S(1)}, u32[]{:S(2)}, u32[]{:S(2)}) collective-permute-start(bf16[1040,128]{1,0:T(8,128)(2,1)S(1)} %copy-done.3), channel_id=1, source_target_pairs={{248,0},{249,1},{0,8},{1,9},{8,16},{9,17},{16,24},{17,25},{24,32},... | collective-permute-start | bytes 798728 | tf_op jit(solution)/shard_map/ppermute | solution.py:299
  58.0 20.1 %collective-permute-start.2 = (bf16[1040,128]{1,0:T(8,128)(2,1)S(1)}, bf16[1040,128]{1,0:T(8,128)(2,1)S(1)}, u32[]{:S(2)}, u32[]{:S(2)}) collective-permute-start(bf16[1040,128]{1,0:T(8,128)(2,1)S(1)} %copy-done.3), channel_id=1, source_target_pairs={{16,0},{241,1},{24,8},{249,9},{32,16},{1,17},{40,24},{9,25},{48,32... | collective-permute-start | bytes 798728 | tf_op jit(solution)/shard_map/ppermute | solution.py:299
  89.3 14.2 %copy-start = (bf16[4,1,16,128]{3,2,1,0:T(8,128)(2,1)S(1)}, bf16[4,1,16,128]{3,2,1,0:T(8,128)(2,1)}, u32[]{:S(2)}) copy-start(bf16[4,1,16,128]{3,2,1,0:T(8,128)(2,1)} %q_ref.1) | copy-start | bytes 49156
  89.3 14.2 %copy-start.1 = (bf16[4,1,2,128]{3,2,1,0:T(2,128)(2,1)S(1)}, bf16[4,1,2,128]{3,2,1,0:T(2,128)(2,1)}, u32[]{:S(2)}) copy-start(bf16[4,1,2,128]{3,2,1,0:T(2,128)(2,1)} %nk_ref.1) | copy-start | bytes 6148
  89.3 14.2 %copy-start.2 = (bf16[4,1,2,128]{3,2,1,0:T(2,128)(2,1)S(1)}, bf16[4,1,2,128]{3,2,1,0:T(2,128)(2,1)}, u32[]{:S(2)}) copy-start(bf16[4,1,2,128]{3,2,1,0:T(2,128)(2,1)} %nv_ref.1) | copy-start | bytes 6148
  89.3 46.1 %all-to-all-start.1 = ((f16[16,40,128]{2,1,0:T(8,128)(2,1)}), f16[16,40,128]{2,1,0:T(8,128)(2,1)S(1)}, u32[]{:S(2)}, u32[]{:S(2)}) async-start(f16[16,40,128]{2,1,0:T(8,128)(2,1)} %convert_element_type.6), calls=%async_computation.1 | async-start | bytes 327680 | tf_op jit(solution)/shard_map/all_to_all | solution.py:315

commit v2 on v1

--- a/solution.py
+++ b/solution.py
@@ -15,6 +15,7 @@
 RING = ("hi", "lo")
 PEERS = ("hi", "row")
 LANES = 128
+EXTRA = 2
 SMALLEST = 2.0**-100
 LOW_SCALE = 1024.0
 
@@ -69,9 +70,10 @@
     copies[0].wait()
     for head in range(heads):
         message = jnp.concatenate(head_queries(q_ref, heads, head) + [masks[head]], axis=0)
-        message = message.astype(ask_ref.dtype)
-        for peer in range(head, ask_ref.shape[0], heads):
-            ask_ref[peer] = message
+        height = message.shape[0] - 8 + EXTRA
+        message = message[0:height].astype(ask_ref.dtype)
+        for peer in range(head, ask_ref.shape[0] // height, heads):
+            ask_ref[peer * height : (peer + 1) * height, :] = message
     for copy in copies[1:3]:
         copy.wait()
     coarse = jnp.concatenate(
@@ -110,10 +112,11 @@
         stat_ref[head] = jnp.where(lane == 0, top, total)
 
 
-def attend(span, near, ring, ask_ref, *rest):
+def attend(span, near, ring, peers, ask_ref, *rest):
     page_refs, reply_ref = rest[:NEAR], rest[NEAR]
-    peers, height, width = ask_ref.shape
-    per_peer = height - 8
+    width = ask_ref.shape[1]
+    height = ask_ref.shape[0] // peers
+    per_peer = height - EXTRA
     scale = 1.0 / math.sqrt(width)
     log_page = math.log(span // near)
     chunk_peers = LANES // per_peer
@@ -144,9 +147,11 @@
     contract_last = (((1,), (1,)), ((), ()))
 
     for chunk in range(peers // chunk_peers):
-        asked = [ask_ref[chunk * chunk_peers + i] for i in range(chunk_peers)]
-        queries = jnp.concatenate([a[:per_peer] for a in asked], axis=0)
-        tails = [a[per_peer:].astype(jnp.float32) for a in asked]
+        first = chunk * chunk_peers * height
+        asked = ask_ref[first : first + chunk_peers * height, :].astype(jnp.float32)
+        asked = [asked[i * height : (i + 1) * height] for i in range(chunk_peers)]
+        queries = jnp.concatenate([a[:per_peer] for a in asked], axis=0).astype(jnp.bfloat16)
+        tails = [a[per_peer:] for a in asked]
         spread = lambda i: jnp.concatenate(
             [jnp.broadcast_to(t[i : i + 1], (per_peer, width)) for t in tails], axis=0
         ).astype(jnp.bfloat16)
@@ -209,24 +214,24 @@
             stats = jnp.where(lane8 == i, part, stats)
         stats = jnp.transpose(stats)[0:8]
         turns = [pltpu.roll(stats, i * per_peer, 1) if i else stats for i in range(chunk_peers)]
-        part_of = lax.broadcasted_iota(jnp.int32, (8, LANES), 1) // per_peer
-        first_row = lax.broadcasted_iota(jnp.int32, (8, LANES), 0) == 0
+        part_of = lax.broadcasted_iota(jnp.int32, (EXTRA, LANES), 1) // per_peer
         for i in range(chunk_peers):
-            peer = chunk * chunk_peers + i
-            reply_ref[peer, 0:per_peer, :] = out[i * per_peer : (i + 1) * per_peer]
-            line = jnp.zeros((8, LANES), jnp.float32)
+            at = first + i * height
+            reply_ref[at : at + per_peer, :] = out[i * per_peer : (i + 1) * per_peer]
+            line = jnp.zeros((EXTRA, LANES), jnp.float32)
             for part in range(chunk_peers):
                 turned = turns[(part - i) % chunk_peers][part : part + 1]
-                line = jnp.where((part_of == part) & first_row, turned, line)
-            reply_ref[peer, per_peer:, :] = line
-
-
-def merge(heads, reply_ref, tail_ref, tail_stat_ref, o_ref):
+                line = jnp.where(part_of == part, turned, line)
+            reply_ref[at + per_peer : at + height, :] = line
+
+
+def merge(heads, peers, reply_ref, tail_ref, tail_stat_ref, o_ref):
     num_steps, _, num_heads, _ = o_ref.shape
     group = num_heads // heads
-    peers, height, _ = reply_ref.shape
-    per_peer = height - 8
-    stats = [reply_ref[p, per_peer : per_peer + 1, :] for p in range(peers)]
+    height = reply_ref.shape[0] // peers
+    per_peer = height - EXTRA
+    replies = [reply_ref[p * height : (p + 1) * height, :] for p in range(peers)]
+    stats = [r[per_peer : per_peer + 1] for r in replies]
     stats = jnp.transpose(
         jnp.concatenate(stats + [jnp.zeros((LANES - peers, LANES), jnp.float32)], axis=0)
     )
@@ -243,7 +248,7 @@
         numer, denom = factor * tail_ref[head], factor * tail_stat_ref[head, :, 1:2]
         for p, top in zip(sources, tops):
             factor = jnp.exp(top - best)
-            numer += (factor * powers[:, p : p + 1]) * reply_ref[p, 0:per_peer, :]
+            numer += (factor * powers[:, p : p + 1]) * replies[p][0:per_peer]
             denom += factor
         results.append(numer / denom)
     for s in range(num_steps):
@@ -269,6 +274,11 @@
     )
 
 
+def exchange(messages, peers):
+    pairs = messages.reshape(peers, -1, 2, messages.shape[1])
+    return lax.all_to_all(pairs, PEERS, 0, 0, tiled=True).reshape(messages.shape)
+
+
 def per_device(ring, queries, new_keys, step_new_values, keys, values, cent_keys, cent_values, slots, picks):
     num_steps, _, num_heads, width = queries.shape
     heads, span = keys.shape[:2]
@@ -276,13 +286,13 @@
     cores = lax.axis_size("row")
     peers = lax.axis_size("hi") * cores
     per_peer = num_steps * num_heads // heads
-    height = per_peer + 8
+    height = per_peer + EXTRA
     shape = jax.ShapeDtypeStruct
     pages, ask = on_core(
         functools.partial(prepare, heads),
         (
             shape((2 * span + 16, width), jnp.bfloat16),
-            shape((peers, height, width), jnp.bfloat16),
+            shape((peers * height, width), jnp.bfloat16),
         ),
         [SMEM] * 2 + [HBM] * 5,
         2**16,
@@ -297,7 +307,7 @@
     for i in range(1, NEAR):
         pairs = shift(lambda c: near_offsets(c)[i])
         fetched.append(lax.ppermute(pages, RING + ("row",), pairs))
-    asked = lax.all_to_all(ask, PEERS, 0, 0, tiled=True)
+    asked = exchange(ask, peers)
     tail_out, tail_stat = on_core(
         functools.partial(tail, heads),
         (shape((heads, per_peer, width), jnp.float32),) * 2,
@@ -306,16 +316,19 @@
         4,
     )(queries, new_keys, step_new_values)
     reply = on_core(
-        functools.partial(attend, span, near, ring),
-        shape((peers, height, width), jnp.float32),
+        functools.partial(attend, span, near, ring, peers),
+        shape((peers * height, width), jnp.float32),
         [VMEM] * (1 + NEAR),
         4 * peers * per_peer * span * NEAR * width,
         20,
     )(asked, *fetched)
-    reply = lax.all_to_all(reply.astype(jnp.float16), PEERS, 0, 0, tiled=True)
-    reply = reply.astype(jnp.float32)
+    reply = exchange(reply.astype(jnp.float16), peers).astype(jnp.float32)
     return on_core(
-        functools.partial(merge, heads), shape(queries.shape, jnp.bfloat16), [VMEM] * 3, 2**20, 8
+        functools.partial(merge, heads, peers),
+        shape(queries.shape, jnp.bfloat16),
+        [VMEM] * 3,
+        2**20,
+        8,
     )(reply, tail_out, tail_stat)
 
 

time: 137 us -> 134 us (0.978)
  waiting for transfers between devices: 54.2 us -> 51.6 us
    all_to_all x2, waiting for transfers between devices: 36.1 us -> 34.7 us  [exchange(): lax.all_to_all(pairs, PEERS, 0, 0, tiled=True).reshape(messages.shape)]
where the time goes in v2:
time: 134 us
  starting transfers between devices  71.4 us (53%)
  waiting for transfers between devices  51.6 us (39%)
  Pallas kernels  10.1 us (8%)
    all_to_all x2, starting transfers between devices, exchange(): lax.all_to_all(pairs, PEERS, 0, 0, tiled=True).reshape(messages.shape)  59.1 us
    all_to_all x2, waiting for transfers between devices, exchange(): lax.all_to_all(pairs, PEERS, 0, 0, tiled=True).reshape(messages.shape)  34.7 us
    ppermute x3, waiting for transfers between devices, per_device(): fetched.append(lax.ppermute(pages, RING + ('row',), pairs))  16.9 us
    ppermute x3, starting transfers between devices, per_device(): fetched.append(lax.ppermute(pages, RING + ('row',), pairs))  12.4 us
    pallas_call x1, Pallas kernels, per_device(): on_core(functools.partial(attend, span, near, ring, peers), shape((peers...  6.15 us
  transfers between devices with their start and end apart: 5, of which 5 were waited for; matrix products, arithmetic and copies ran while one was open for 0% of the time, Pallas kernels for 0%

profile of v2, /device:TPU:33, one launch (start us, length us, event | category | flops | bytes accessed | tf_op | source)
XLA Modules:
  0.0 134.0 jit_solution(6460614959476287133)
XLA Ops:
  0.0 2.5 %shard_map.91 = (bf16[1040,128]{1,0:T(8,128)(2,1)}, bf16[544,128]{1,0:T(8,128)(2,1)}) custom-call(s32[1,2,16]{2,1,0:T(2,128)} %picks_ref.1, s32[2,128]{1,0:T(2,128)} %slots_ref.1, bf16[4,1,16,128]{3,2,1,0:T(8,128)(2,1)} %q_ref.1, bf16[2,512,128]{2,1,0:T(8,128)(2,1)} %k_ref.1, bf16[2,512,128]{2,1,0:T(8,128)(2,1)} %v_ref.1, bf16[2,4,128]{2,1,0:T(4,128)(2,1)} %ck_ref.1, ...), custom_call_target="tpu_custom_call" | custom-call | flops 65536 | bytes 1048576 | tf_op jit(solution)/shard_map/pallas_call | solution.py:291
  2.5 0.0 copy-start.3
  2.5 45.0 %all-to-all-start = ((bf16[16,17,2,128]{3,2,1,0:T(2,128)(2,1)}), bf16[16,17,2,128]{3,2,1,0:T(2,128)(2,1)S(1)}, u32[]{:S(2)}, u32[]{:S(2)}) async-start(bf16[16,17,2,128]{3,2,1,0:T(2,128)(2,1)} %bitcast.7), calls=%async_computation | async-start | bytes 278528 | tf_op jit(solution)/shard_map/all_to_all | solution.py:279
  47.5 0.0 copy-done.3
  47.6 8.4 %collective-permute-start = (bf16[1040,128]{1,0:T(8,128)(2,1)S(1)}, bf16[1040,128]{1,0:T(8,128)(2,1)S(1)}, u32[]{:S(2)}, u32[]{:S(2)}) collective-permute-start(bf16[1040,128]{1,0:T(8,128)(2,1)S(1)} %copy-done.3), channel_id=1, source_target_pairs={{8,0},{9,1},{16,8},{17,9},{24,16},{25,17},{32,24},{33,25},{40,32},... | collective-permute-start | bytes 798728 | tf_op jit(solution)/shard_map/ppermute | solution.py:309
  56.0 2.0 %collective-permute-start.1 = (bf16[1040,128]{1,0:T(8,128)(2,1)S(1)}, bf16[1040,128]{1,0:T(8,128)(2,1)S(1)}, u32[]{:S(2)}, u32[]{:S(2)}) collective-permute-start(bf16[1040,128]{1,0:T(8,128)(2,1)S(1)} %copy-done.3), channel_id=1, source_target_pairs={{248,0},{249,1},{0,8},{1,9},{8,16},{9,17},{16,24},{17,25},{24,32},... | collective-permute-start | bytes 798728 | tf_op jit(solution)/shard_map/ppermute | solution.py:309
  58.0 2.0 %collective-permute-start.2 = (bf16[1040,128]{1,0:T(8,128)(2,1)S(1)}, bf16[1040,128]{1,0:T(8,128)(2,1)S(1)}, u32[]{:S(2)}, u32[]{:S(2)}) collective-permute-start(bf16[1040,128]{1,0:T(8,128)(2,1)S(1)} %copy-done.3), channel_id=1, source_target_pairs={{16,0},{241,1},{24,8},{249,9},{32,16},{1,17},{40,24},{9,25},{48,32... | collective-permute-start | bytes 798728 | tf_op jit(solution)/shard_map/ppermute | solution.py:309
  59.9 7.7 %collective-permute-done.rest_1_ = bf16[1040,128]{1,0:T(8,128)(2,1)S(1)} collective-permute-done((bf16[1040,128]{1,0:T(8,128)(2,1)S(1)}, bf16[1040,128]{1,0:T(8,128)(2,1)S(1)}, u32[]{:S(2)}, u32[]{:S(2)}) %collective-permute-start) | collective-permute-done | bytes 266272 | tf_op jit(solution)/shard_map/ppermute | solution.py:309
  67.6 3.7 %collective-permute-done.1.rest_2_ = bf16[1040,128]{1,0:T(8,128)(2,1)S(1)} collective-permute-done((bf16[1040,128]{1,0:T(8,128)(2,1)S(1)}, bf16[1040,128]{1,0:T(8,128)(2,1)S(1)}, u32[]{:S(2)}, u32[]{:S(2)}) %collective-permute-start.1) | collective-permute-done | bytes 266272 | tf_op jit(solution)/shard_map/ppermute | solution.py:309
  71.3 5.5 %collective-permute-done.2.rest_3_ = bf16[1040,128]{1,0:T(8,128)(2,1)S(1)} collective-permute-done((bf16[1040,128]{1,0:T(8,128)(2,1)S(1)}, bf16[1040,128]{1,0:T(8,128)(2,1)S(1)}, u32[]{:S(2)}, u32[]{:S(2)}) %collective-permute-start.2) | collective-permute-done | bytes 266272 | tf_op jit(solution)/shard_map/ppermute | solution.py:309
  76.9 3.5 %all-to-all-done = bf16[16,17,2,128]{3,2,1,0:T(2,128)(2,1)S(1)} async-done(((bf16[16,17,2,128]{3,2,1,0:T(2,128)(2,1)}), bf16[16,17,2,128]{3,2,1,0:T(2,128)(2,1)S(1)}, u32[]{:S(2)}, u32[]{:S(2)}) %all-to-all-start) | async-done | bytes 139296 | tf_op jit(solution)/shard_map/all_to_all | solution.py:279
  80.3 6.1 %shard_map.92 = f32[544,128]{1,0:T(8,128)S(1)} custom-call(bf16[544,128]{1,0:T(8,128)(2,1)S(1)} %bitcast.5, bf16[1040,128]{1,0:T(8,128)(2,1)S(1)} %copy-done.3, bf16[1040,128]{1,0:T(8,128)(2,1)S(1)} %collective-permute-done.rest_1_, bf16[1040,128]{1,0:T(8,128)(2,1)S(1)} %collective-permute-done.1.rest_2_, bf16[1040,128]{1,0:T(8,128)(2,1)S(1)} %collective-permute-done.2.rest_3_), custom_call_target="tpu_custom_call" | custom-call | flops 536870912 | bytes 1048576 | tf_op jit(solution)/shard_map/pallas_call | solution.py:318
  86.5 0.7 convert_element_type.8
  87.2 0.0 copy-start
  87.2 0.0 copy-start.1
  87.2 0.0 copy-start.2
  87.2 14.1 %all-to-all-start.1 = ((f16[16,17,2,128]{3,2,1,0:T(2,128)(2,1)}), f16[16,17,2,128]{3,2,1,0:T(2,128)(2,1)S(1)}, u32[]{:S(2)}, u32[]{:S(2)}) async-start(f16[16,17,2,128]{3,2,1,0:T(2,128)(2,1)} %bitcast.2), calls=%async_computation.1 | async-start | bytes 278528 | tf_op jit(solution)/shard_map/all_to_all | solution.py:279
  101.3 0.0 copy-done
  101.3 0.0 copy-done.1
  101.3 0.0 copy-done.2
  101.3 0.1 shard_map.93
  101.4 31.2 %all-to-all-done.1 = f16[16,17,2,128]{3,2,1,0:T(2,128)(2,1)S(1)} async-done(((f16[16,17,2,128]{3,2,1,0:T(2,128)(2,1)}), f16[16,17,2,128]{3,2,1,0:T(2,128)(2,1)S(1)}, u32[]{:S(2)}, u32[]{:S(2)}) %all-to-all-start.1) | async-done | bytes 139296 | tf_op jit(solution)/shard_map/all_to_all | solution.py:279
  132.7 1.3 shard_map.94
  (1 shorter events, 0.0 us)
Async XLA Ops:
  2.5 45.0 %copy-start.3 = (bf16[1040,128]{1,0:T(8,128)(2,1)S(1)}, bf16[1040,128]{1,0:T(8,128)(2,1)}, u32[]{:S(2)}) copy-start(bf16[1040,128]{1,0:T(8,128)(2,1)} %get-tuple-element.10.rest_0_) | copy-start | bytes 798724
  2.5 77.8 %all-to-all-start = ((bf16[16,17,2,128]{3,2,1,0:T(2,128)(2,1)}), bf16[16,17,2,128]{3,2,1,0:T(2,128)(2,1)S(1)}, u32[]{:S(2)}, u32[]{:S(2)}) async-start(bf16[16,17,2,128]{3,2,1,0:T(2,128)(2,1)} %bitcast.7), calls=%async_computation | async-start | bytes 278528 | tf_op jit(solution)/shard_map/all_to_all | solution.py:279
  47.6 20.0 %collective-permute-start = (bf16[1040,128]{1,0:T(8,128)(2,1)S(1)}, bf16[1040,128]{1,0:T(8,128)(2,1)S(1)}, u32[]{:S(2)}, u32[]{:S(2)}) collective-permute-start(bf16[1040,128]{1,0:T(8,128)(2,1)S(1)} %copy-done.3), channel_id=1, source_target_pairs={{8,0},{9,1},{16,8},{17,9},{24,16},{25,17},{32,24},{33,25},{40,32},... | collective-permute-start | bytes 798728 | tf_op jit(solution)/shard_map/ppermute | solution.py:309
  56.0 15.3 %collective-permute-start.1 = (bf16[1040,128]{1,0:T(8,128)(2,1)S(1)}, bf16[1040,128]{1,0:T(8,128)(2,1)S(1)}, u32[]{:S(2)}, u32[]{:S(2)}) collective-permute-start(bf16[1040,128]{1,0:T(8,128)(2,1)S(1)} %copy-done.3), channel_id=1, source_target_pairs={{248,0},{249,1},{0,8},{1,9},{8,16},{9,17},{16,24},{17,25},{24,32},... | collective-permute-start | bytes 798728 | tf_op jit(solution)/shard_map/ppermute | solution.py:309
  58.0 18.9 %collective-permute-start.2 = (bf16[1040,128]{1,0:T(8,128)(2,1)S(1)}, bf16[1040,128]{1,0:T(8,128)(2,1)S(1)}, u32[]{:S(2)}, u32[]{:S(2)}) collective-permute-start(bf16[1040,128]{1,0:T(8,128)(2,1)S(1)} %copy-done.3), channel_id=1, source_target_pairs={{16,0},{241,1},{24,8},{249,9},{32,16},{1,17},{40,24},{9,25},{48,32... | collective-permute-start | bytes 798728 | tf_op jit(solution)/shard_map/ppermute | solution.py:309
  87.2 14.1 %copy-start = (bf16[4,1,16,128]{3,2,1,0:T(8,128)(2,1)S(1)}, bf16[4,1,16,128]{3,2,1,0:T(8,128)(2,1)}, u32[]{:S(2)}) copy-start(bf16[4,1,16,128]{3,2,1,0:T(8,128)(2,1)} %q_ref.1) | copy-start | bytes 49156
  87.2 14.1 %copy-start.1 = (bf16[4,1,2,128]{3,2,1,0:T(2,128)(2,1)S(1)}, bf16[4,1,2,128]{3,2,1,0:T(2,128)(2,1)}, u32[]{:S(2)}) copy-start(bf16[4,1,2,128]{3,2,1,0:T(2,128)(2,1)} %nk_ref.1) | copy-start | bytes 6148
  87.2 14.1 %copy-start.2 = (bf16[4,1,2,128]{3,2,1,0:T(2,128)(2,1)S(1)}, bf16[4,1,2,128]{3,2,1,0:T(2,128)(2,1)}, u32[]{:S(2)}) copy-start(bf16[4,1,2,128]{3,2,1,0:T(2,128)(2,1)} %nv_ref.1) | copy-start | bytes 6148
  87.2 45.4 %all-to-all-start.1 = ((f16[16,17,2,128]{3,2,1,0:T(2,128)(2,1)}), f16[16,17,2,128]{3,2,1,0:T(2,128)(2,1)S(1)}, u32[]{:S(2)}, u32[]{:S(2)}) async-start(f16[16,17,2,128]{3,2,1,0:T(2,128)(2,1)} %bitcast.2), calls=%async_computation.1 | async-start | bytes 278528 | tf_op jit(solution)/shard_map/all_to_all | solution.py:279

commit v3 on v2

--- a/solution.py
+++ b/solution.py
@@ -18,6 +18,8 @@
 EXTRA = 2
 SMALLEST = 2.0**-100
 LOW_SCALE = 1024.0
+LOG2_E = math.log2(math.e)
+CHUNK = 256
 
 
 def as_bf16(x):
@@ -112,117 +114,120 @@
         stat_ref[head] = jnp.where(lane == 0, top, total)
 
 
-def attend(span, near, ring, peers, ask_ref, *rest):
-    page_refs, reply_ref = rest[:NEAR], rest[NEAR]
-    width = ask_ref.shape[1]
-    height = ask_ref.shape[0] // peers
-    per_peer = height - EXTRA
-    scale = 1.0 / math.sqrt(width)
-    log_page = math.log(span // near)
-    chunk_peers = LANES // per_peer
+def arrange(span, near, ring, *refs):
+    page_refs, (keys_ref, values_ref, ends_ref, end_values_ref) = refs[:NEAR], refs[NEAR:]
+    width = page_refs[0].shape[1]
     position, core = place()
     shards = [lax.rem(position + off + ring, ring) for off in near_offsets(core)]
     page = span // near
     lane = lax.broadcasted_iota(jnp.int32, (page, width), 1)
-    keys = []
-    for ref, shard in zip(page_refs, shards):
-        picker = jnp.concatenate(
-            [jnp.where(lane == shard * near + p, MASKED, 0.0) for p in range(near)], axis=0
-        ).astype(jnp.bfloat16)
-        keys.append(jnp.concatenate([ref[0:span, :], picker], axis=1))
+    row = lax.broadcasted_iota(jnp.int32, (NEAR * near, width), 0)
+    column = lax.broadcasted_iota(jnp.int32, (NEAR * near, width), 1)
+    cluster = jnp.full((NEAR * near, width), -1, jnp.int32)
+    for b, (ref, shard) in enumerate(zip(page_refs, shards)):
+        keys_ref[b, :, 0:width] = ref[0:span, :]
+        for p in range(near):
+            picker = jnp.where(lane == shard * near + p, MASKED, 0.0)
+            keys_ref[b, p * page : (p + 1) * page, width:] = picker.astype(jnp.bfloat16)
+        values_ref[b] = jnp.transpose(ref[span : 2 * span, :])
+        cluster = jnp.where(row // near == b, shard * near + row - b * near, cluster)
     ends = [ref[2 * span :, :].astype(jnp.float32) for ref in page_refs]
+    picker = jnp.where(column == cluster, MASKED, 0.0)
+    coarse = jnp.concatenate([e[0:near] for e in ends], axis=0)
+    ends_ref[...] = jnp.concatenate([coarse, picker], axis=1).astype(jnp.bfloat16)
     blank = jnp.zeros((LANES - near * NEAR, width), jnp.float32)
-    coarse_keys = jnp.concatenate([e[0:near] for e in ends] + [blank], axis=0)
-    coarse_values = jnp.concatenate([e[near : 2 * near] for e in ends] + [blank], axis=0)
-    coarse_values = coarse_values.astype(jnp.bfloat16)
-    row = lax.broadcasted_iota(jnp.int32, (LANES, width), 0)
-    column = lax.broadcasted_iota(jnp.int32, (LANES, width), 1)
-    cluster = jnp.full((LANES, width), -1, jnp.int32)
-    for b, shard in enumerate(shards):
-        cluster = jnp.where(row // near == b, shard * near + row - b * near, cluster)
-    picker = jnp.where(column == cluster, MASKED, 0.0)
-    coarse_keys = jnp.concatenate([coarse_keys, picker], axis=1).astype(jnp.bfloat16)
-    block_of = lax.broadcasted_iota(jnp.int32, (LANES, LANES), 1) // near
-    lane8 = lax.broadcasted_iota(jnp.int32, (LANES, LANES), 1)
+    coarse = jnp.concatenate([e[near : 2 * near] for e in ends] + [blank], axis=0)
+    end_values_ref[...] = jnp.transpose(coarse)[:, 0 : near * NEAR].astype(jnp.bfloat16)
+
+
+def attend(span, near, peers, ask_ref, keys_ref, values_ref, ends_ref, end_values_ref, reply_ref):
+    width = ask_ref.shape[1]
+    height = ask_ref.shape[0] // peers
+    per_peer = height - EXTRA
+    scale = LOG2_E / math.sqrt(width)
+    log_page = math.log2(span // near)
+    floor = FLOOR_SCORE * LOG2_E
+    chunk_peers = CHUNK // per_peer
+    parts = LANES // per_peer
     contract_last = (((1,), (1,)), ((), ()))
+    block_of = lax.broadcasted_iota(jnp.int32, (NEAR * near, CHUNK), 0) // near
+    part_of = lax.broadcasted_iota(jnp.int32, (EXTRA, LANES), 1) // per_peer
+    sub = lax.broadcasted_iota(jnp.int32, (8, CHUNK), 0)
+    ends = ends_ref[...]
+    end_values = end_values_ref[...]
 
     for chunk in range(peers // chunk_peers):
         first = chunk * chunk_peers * height
         asked = ask_ref[first : first + chunk_peers * height, :].astype(jnp.float32)
         asked = [asked[i * height : (i + 1) * height] for i in range(chunk_peers)]
         queries = jnp.concatenate([a[:per_peer] for a in asked], axis=0).astype(jnp.bfloat16)
-        tails = [a[per_peer:] for a in asked]
         spread = lambda i: jnp.concatenate(
-            [jnp.broadcast_to(t[i : i + 1], (per_peer, width)) for t in tails], axis=0
+            [jnp.broadcast_to(a[per_peer + i :][0:1], (per_peer, width)) for a in asked], axis=0
         ).astype(jnp.bfloat16)
         exact_queries = jnp.concatenate([queries, spread(0)], axis=1)
         coarse_queries = jnp.concatenate([queries, spread(1)], axis=1)
-        coarse = (
-            lax.dot_general(
-                coarse_queries, coarse_keys, contract_last, preferred_element_type=jnp.float32
-            )
-            * scale
-            + log_page
+        coarse = lax.dot_general(
+            ends, coarse_queries, contract_last, preferred_element_type=jnp.float32
         )
+        coarse = coarse * scale + log_page
         tops, totals, outs = [], [], []
         for b in range(NEAR):
-            scores = (
-                lax.dot_general(
-                    exact_queries, keys[b], contract_last, preferred_element_type=jnp.float32
-                )
-                * scale
+            scores = lax.dot_general(
+                keys_ref[b], exact_queries, contract_last, preferred_element_type=jnp.float32
             )
             mine = block_of == b
             top = jnp.maximum(
-                jnp.max(scores, axis=1, keepdims=True),
-                jnp.max(jnp.where(mine, coarse, FLOOR_SCORE), axis=1, keepdims=True),
+                jnp.max(scores, axis=0, keepdims=True) * scale,
+                jnp.max(jnp.where(mine, coarse, floor), axis=0, keepdims=True),
             )
-            top = jnp.maximum(top, FLOOR_SCORE)
-            weights = jnp.exp(scores - top)
-            coarse_weights = jnp.where(mine, jnp.exp(jnp.where(mine, coarse - top, 0.0)), 0.0)
+            top = jnp.maximum(top, floor)
+            weights = jnp.exp2(scores * scale - top)
+            coarse_weights = jnp.where(mine, jnp.exp2(jnp.where(mine, coarse - top, 0.0)), 0.0)
             totals.append(
-                jnp.sum(weights, axis=1, keepdims=True)
-                + jnp.sum(coarse_weights, axis=1, keepdims=True)
+                jnp.sum(weights, axis=0, keepdims=True)
+                + jnp.sum(coarse_weights, axis=0, keepdims=True)
             )
             outs.append(
                 jnp.dot(
+                    values_ref[b],
                     weights.astype(jnp.bfloat16),
-                    page_refs[b][span : 2 * span, :],
                     preferred_element_type=jnp.float32,
                 )
                 + jnp.dot(
+                    end_values,
                     coarse_weights.astype(jnp.bfloat16),
-                    coarse_values,
                     preferred_element_type=jnp.float32,
                 )
             )
             tops.append(top)
         best = functools.reduce(jnp.maximum, tops)
-        factors = [jnp.exp(t - best) for t in tops]
+        factors = [jnp.exp2(t - best) for t in tops]
         total = sum(f * t for f, t in zip(factors, totals))
         out = sum(f * o for f, o in zip(factors, outs))
-        level = jnp.where(total > 0.0, best + jnp.log(total), 2 * FLOOR_SCORE)
-        out = out * jnp.where(total > 0.0, 1.0 / total, 0.0)
-        largest = jnp.max(jnp.abs(out), axis=1, keepdims=True)
+        some = total > 0.0
+        level = jnp.where(some, best + jnp.log2(jnp.where(some, total, 1.0)), 2 * floor)
+        out = out * jnp.where(some, 1.0 / jnp.where(some, total, 1.0), 0.0)
+        largest = jnp.max(jnp.abs(out), axis=0, keepdims=True)
         power = jnp.ceil(jnp.log2(jnp.maximum(largest, SMALLEST)))
-        out = out * jnp.exp2(-power)
+        out = jnp.transpose(out * jnp.exp2(-power))
         high = as_bf16(level)
         middle = as_bf16(level - high)
         low = (level - high - middle) * LOW_SCALE
-        stats = jnp.zeros((LANES, LANES), jnp.float32)
+        stats = jnp.zeros((8, CHUNK), jnp.float32)
         for i, part in enumerate((high, middle, low, power)):
-            stats = jnp.where(lane8 == i, part, stats)
-        stats = jnp.transpose(stats)[0:8]
-        turns = [pltpu.roll(stats, i * per_peer, 1) if i else stats for i in range(chunk_peers)]
-        part_of = lax.broadcasted_iota(jnp.int32, (EXTRA, LANES), 1) // per_peer
-        for i in range(chunk_peers):
-            at = first + i * height
-            reply_ref[at : at + per_peer, :] = out[i * per_peer : (i + 1) * per_peer]
-            line = jnp.zeros((EXTRA, LANES), jnp.float32)
-            for part in range(chunk_peers):
-                turned = turns[(part - i) % chunk_peers][part : part + 1]
-                line = jnp.where(part_of == part, turned, line)
-            reply_ref[at + per_peer : at + height, :] = line
+            stats = jnp.where(sub == i, part, stats)
+        for half in range(CHUNK // LANES):
+            held = stats[:, half * LANES : (half + 1) * LANES]
+            turns = [pltpu.roll(held, i * per_peer, 1) if i else held for i in range(parts)]
+            for i in range(parts):
+                peer = half * parts + i
+                at = first + peer * height
+                reply_ref[at : at + per_peer, :] = out[peer * per_peer : (peer + 1) * per_peer]
+                line = jnp.zeros((EXTRA, LANES), jnp.float32)
+                for part in range(parts):
+                    turned = turns[(part - i) % parts][part : part + 1]
+                    line = jnp.where(part_of == part, turned, line)
+                reply_ref[at + per_peer : at + height, :] = line
 
 
 def merge(heads, peers, reply_ref, tail_ref, tail_stat_ref, o_ref):
@@ -242,12 +247,12 @@
     for head in range(heads):
         sources = range(head, peers, heads)
         tops = [levels[:, p : p + 1] for p in sources]
-        tail_top = tail_stat_ref[head, :, 0:1]
+        tail_top = tail_stat_ref[head, :, 0:1] * LOG2_E
         best = functools.reduce(jnp.maximum, tops, tail_top)
-        factor = jnp.exp(tail_top - best)
+        factor = jnp.exp2(tail_top - best)
         numer, denom = factor * tail_ref[head], factor * tail_stat_ref[head, :, 1:2]
         for p, top in zip(sources, tops):
-            factor = jnp.exp(top - best)
+            factor = jnp.exp2(top - best)
             numer += (factor * powers[:, p : p + 1]) * replies[p][0:per_peer]
             denom += factor
         results.append(numer / denom)
@@ -315,13 +320,25 @@
         2**22,
         4,
     )(queries, new_keys, step_new_values)
+    arranged = on_core(
+        functools.partial(arrange, span, near, ring),
+        (
+            shape((NEAR, span, 2 * width), jnp.bfloat16),
+            shape((NEAR, width, span), jnp.bfloat16),
+            shape((NEAR * near, 2 * width), jnp.bfloat16),
+            shape((width, NEAR * near), jnp.bfloat16),
+        ),
+        [VMEM] * NEAR,
+        2**22,
+        20,
+    )(*fetched)
     reply = on_core(
-        functools.partial(attend, span, near, ring, peers),
+        functools.partial(attend, span, near, peers),
         shape((peers * height, width), jnp.float32),
-        [VMEM] * (1 + NEAR),
+        [VMEM] * 5,
         4 * peers * per_peer * span * NEAR * width,
         20,
-    )(asked, *fetched)
+    )(asked, *arranged)
     reply = exchange(reply.astype(jnp.float16), peers).astype(jnp.float32)
     return on_core(
         functools.partial(merge, heads, peers),

time: 134 us -> 131 us (0.978)
  Pallas kernels: 10.1 us -> 7.17 us
    pallas_call x1 -> x2, Pallas kernels: 6.15 us -> 3.21 us  [the longest x1 2.94 us: per_device(): on_core(functools.partial(attend, span, near, peers), shape((peers * heig...]
where the time goes in v3:
time: 131 us
  starting transfers between devices  71.7 us (55%)
  waiting for transfers between devices  51.3 us (39%)
  Pallas kernels  7.17 us (5%)
    all_to_all x2, starting transfers between devices, exchange(): lax.all_to_all(pairs, PEERS, 0, 0, tiled=True).reshape(messages.shape)  59.4 us
    all_to_all x2, waiting for transfers between devices, exchange(): lax.all_to_all(pairs, PEERS, 0, 0, tiled=True).reshape(messages.shape)  34.3 us
    ppermute x3, waiting for transfers between devices, per_device(): fetched.append(lax.ppermute(pages, RING + ('row',), pairs))  16.9 us
    ppermute x3, starting transfers between devices, per_device(): fetched.append(lax.ppermute(pages, RING + ('row',), pairs))  12.4 us
    pallas_call x1, Pallas kernels, per_device(): on_core(functools.partial(attend, span, near, peers), shape((peers * heig...  2.94 us
  transfers between devices with their start and end apart: 5, of which 5 were waited for; matrix products, arithmetic and copies ran while one was open for 0% of the time, Pallas kernels for 0%

profile of v3, /device:TPU:33, one launch (start us, length us, event | category | flops | bytes accessed | tf_op | source)
XLA Modules:
  0.0 131.0 jit_solution(5726502793078257288)
XLA Ops:
  0.0 2.5 %shard_map.91 = (bf16[1040,128]{1,0:T(8,128)(2,1)}, bf16[544,128]{1,0:T(8,128)(2,1)}) custom-call(s32[1,2,16]{2,1,0:T(2,128)} %picks_ref.1, s32[2,128]{1,0:T(2,128)} %slots_ref.1, bf16[4,1,16,128]{3,2,1,0:T(8,128)(2,1)} %q_ref.1, bf16[2,512,128]{2,1,0:T(8,128)(2,1)} %k_ref.1, bf16[2,512,128]{2,1,0:T(8,128)(2,1)} %v_ref.1, bf16[2,4,128]{2,1,0:T(4,128)(2,1)} %ck_ref.1, ...), custom_call_target="tpu_custom_call" | custom-call | flops 65536 | bytes 1048576 | tf_op jit(solution)/shard_map/pallas_call | solution.py:296
  2.5 0.0 copy-start
  2.5 45.0 %all-to-all-start = ((bf16[16,17,2,128]{3,2,1,0:T(2,128)(2,1)}), bf16[16,17,2,128]{3,2,1,0:T(2,128)(2,1)S(1)}, u32[]{:S(2)}, u32[]{:S(2)}) async-start(bf16[16,17,2,128]{3,2,1,0:T(2,128)(2,1)} %bitcast.7), calls=%async_computation | async-start | bytes 278528 | tf_op jit(solution)/shard_map/all_to_all | solution.py:284
  47.6 0.0 copy-done
  47.6 8.4 %collective-permute-start = (bf16[1040,128]{1,0:T(8,128)(2,1)S(1)}, bf16[1040,128]{1,0:T(8,128)(2,1)S(1)}, u32[]{:S(2)}, u32[]{:S(2)}) collective-permute-start(bf16[1040,128]{1,0:T(8,128)(2,1)S(1)} %copy-done), channel_id=1, source_target_pairs={{8,0},{9,1},{16,8},{17,9},{24,16},{25,17},{32,24},{33,25},{40,32},... | collective-permute-start | bytes 798728 | tf_op jit(solution)/shard_map/ppermute | solution.py:314
  56.0 2.0 %collective-permute-start.1 = (bf16[1040,128]{1,0:T(8,128)(2,1)S(1)}, bf16[1040,128]{1,0:T(8,128)(2,1)S(1)}, u32[]{:S(2)}, u32[]{:S(2)}) collective-permute-start(bf16[1040,128]{1,0:T(8,128)(2,1)S(1)} %copy-done), channel_id=1, source_target_pairs={{248,0},{249,1},{0,8},{1,9},{8,16},{9,17},{16,24},{17,25},{24,32},... | collective-permute-start | bytes 798728 | tf_op jit(solution)/shard_map/ppermute | solution.py:314
  58.0 2.0 %collective-permute-start.2 = (bf16[1040,128]{1,0:T(8,128)(2,1)S(1)}, bf16[1040,128]{1,0:T(8,128)(2,1)S(1)}, u32[]{:S(2)}, u32[]{:S(2)}) collective-permute-start(bf16[1040,128]{1,0:T(8,128)(2,1)S(1)} %copy-done), channel_id=1, source_target_pairs={{16,0},{241,1},{24,8},{249,9},{32,16},{1,17},{40,24},{9,25},{48,32... | collective-permute-start | bytes 798728 | tf_op jit(solution)/shard_map/ppermute | solution.py:314
  59.9 7.7 %collective-permute-done.refs_1_ = bf16[1040,128]{1,0:T(8,128)(2,1)S(1)} collective-permute-done((bf16[1040,128]{1,0:T(8,128)(2,1)S(1)}, bf16[1040,128]{1,0:T(8,128)(2,1)S(1)}, u32[]{:S(2)}, u32[]{:S(2)}) %collective-permute-start) | collective-permute-done | bytes 266272 | tf_op jit(solution)/shard_map/ppermute | solution.py:314
  67.6 3.7 %collective-permute-done.1.refs_2_ = bf16[1040,128]{1,0:T(8,128)(2,1)S(1)} collective-permute-done((bf16[1040,128]{1,0:T(8,128)(2,1)S(1)}, bf16[1040,128]{1,0:T(8,128)(2,1)S(1)}, u32[]{:S(2)}, u32[]{:S(2)}) %collective-permute-start.1) | collective-permute-done | bytes 266272 | tf_op jit(solution)/shard_map/ppermute | solution.py:314
  71.4 5.5 %collective-permute-done.2.refs_3_ = bf16[1040,128]{1,0:T(8,128)(2,1)S(1)} collective-permute-done((bf16[1040,128]{1,0:T(8,128)(2,1)S(1)}, bf16[1040,128]{1,0:T(8,128)(2,1)S(1)}, u32[]{:S(2)}, u32[]{:S(2)}) %collective-permute-start.2) | collective-permute-done | bytes 266272 | tf_op jit(solution)/shard_map/ppermute | solution.py:314
  76.9 0.3 shard_map.92
  77.2 3.2 %all-to-all-done = bf16[16,17,2,128]{3,2,1,0:T(2,128)(2,1)S(1)} async-done(((bf16[16,17,2,128]{3,2,1,0:T(2,128)(2,1)}), bf16[16,17,2,128]{3,2,1,0:T(2,128)(2,1)S(1)}, u32[]{:S(2)}, u32[]{:S(2)}) %all-to-all-start) | async-done | bytes 139296 | tf_op jit(solution)/shard_map/all_to_all | solution.py:284
  80.4 2.9 %shard_map.93 = f32[544,128]{1,0:T(8,128)S(1)} custom-call(bf16[544,128]{1,0:T(8,128)(2,1)S(1)} %bitcast.5, bf16[4,512,256]{2,1,0:T(8,128)(2,1)S(1)} %get-tuple-element.15.keys_ref, bf16[4,128,512]{2,1,0:T(8,128)(2,1)S(1)} %get-tuple-element.16.values_ref, bf16[16,256]{1,0:T(8,128)(2,1)S(1)} %get-tuple-element.17.ends_ref, ...), custom_call_target="tpu_custom_call" | custom-call | flops 536870912 | bytes 1048576 | tf_op jit(solution)/shard_map/pallas_call | solution.py:335
  83.3 0.7 convert_element_type.8
  84.0 0.0 copy-start.1
  84.0 0.0 copy-start.2
  84.0 0.0 copy-start.3
  84.0 14.3 %all-to-all-start.1 = ((f16[16,17,2,128]{3,2,1,0:T(2,128)(2,1)}), f16[16,17,2,128]{3,2,1,0:T(2,128)(2,1)S(1)}, u32[]{:S(2)}, u32[]{:S(2)}) async-start(f16[16,17,2,128]{3,2,1,0:T(2,128)(2,1)} %bitcast.2), calls=%async_computation.1 | async-start | bytes 278528 | tf_op jit(solution)/shard_map/all_to_all | solution.py:284
  98.3 0.0 copy-done.1
  98.3 0.0 copy-done.2
  98.4 0.0 copy-done.3
  98.4 0.1 shard_map.94
  98.5 31.2 %all-to-all-done.1 = f16[16,17,2,128]{3,2,1,0:T(2,128)(2,1)S(1)} async-done(((f16[16,17,2,128]{3,2,1,0:T(2,128)(2,1)}), f16[16,17,2,128]{3,2,1,0:T(2,128)(2,1)S(1)}, u32[]{:S(2)}, u32[]{:S(2)}) %all-to-all-start.1) | async-done | bytes 139296 | tf_op jit(solution)/shard_map/all_to_all | solution.py:284
  129.7 1.3 shard_map.95
  (1 shorter events, 0.0 us)
Async XLA Ops:
  2.5 45.0 %copy-start = (bf16[1040,128]{1,0:T(8,128)(2,1)S(1)}, bf16[1040,128]{1,0:T(8,128)(2,1)}, u32[]{:S(2)}) copy-start(bf16[1040,128]{1,0:T(8,128)(2,1)} %get-tuple-element.14.refs_0_) | copy-start | bytes 798724
  2.5 77.8 %all-to-all-start = ((bf16[16,17,2,128]{3,2,1,0:T(2,128)(2,1)}), bf16[16,17,2,128]{3,2,1,0:T(2,128)(2,1)S(1)}, u32[]{:S(2)}, u32[]{:S(2)}) async-start(bf16[16,17,2,128]{3,2,1,0:T(2,128)(2,1)} %bitcast.7), calls=%async_computation | async-start | bytes 278528 | tf_op jit(solution)/shard_map/all_to_all | solution.py:284
  47.6 20.0 %collective-permute-start = (bf16[1040,128]{1,0:T(8,128)(2,1)S(1)}, bf16[1040,128]{1,0:T(8,128)(2,1)S(1)}, u32[]{:S(2)}, u32[]{:S(2)}) collective-permute-start(bf16[1040,128]{1,0:T(8,128)(2,1)S(1)} %copy-done), channel_id=1, source_target_pairs={{8,0},{9,1},{16,8},{17,9},{24,16},{25,17},{32,24},{33,25},{40,32},... | collective-permute-start | bytes 798728 | tf_op jit(solution)/shard_map/ppermute | solution.py:314
  56.0 15.3 %collective-permute-start.1 = (bf16[1040,128]{1,0:T(8,128)(2,1)S(1)}, bf16[1040,128]{1,0:T(8,128)(2,1)S(1)}, u32[]{:S(2)}, u32[]{:S(2)}) collective-permute-start(bf16[1040,128]{1,0:T(8,128)(2,1)S(1)} %copy-done), channel_id=1, source_target_pairs={{248,0},{249,1},{0,8},{1,9},{8,16},{9,17},{16,24},{17,25},{24,32},... | collective-permute-start | bytes 798728 | tf_op jit(solution)/shard_map/ppermute | solution.py:314
  58.0 18.9 %collective-permute-start.2 = (bf16[1040,128]{1,0:T(8,128)(2,1)S(1)}, bf16[1040,128]{1,0:T(8,128)(2,1)S(1)}, u32[]{:S(2)}, u32[]{:S(2)}) collective-permute-start(bf16[1040,128]{1,0:T(8,128)(2,1)S(1)} %copy-done), channel_id=1, source_target_pairs={{16,0},{241,1},{24,8},{249,9},{32,16},{1,17},{40,24},{9,25},{48,32... | collective-permute-start | bytes 798728 | tf_op jit(solution)/shard_map/ppermute | solution.py:314
  84.0 14.4 %copy-start.1 = (bf16[4,1,16,128]{3,2,1,0:T(8,128)(2,1)S(1)}, bf16[4,1,16,128]{3,2,1,0:T(8,128)(2,1)}, u32[]{:S(2)}) copy-start(bf16[4,1,16,128]{3,2,1,0:T(8,128)(2,1)} %q_ref.1) | copy-start | bytes 49156
  84.0 14.4 %copy-start.2 = (bf16[4,1,2,128]{3,2,1,0:T(2,128)(2,1)S(1)}, bf16[4,1,2,128]{3,2,1,0:T(2,128)(2,1)}, u32[]{:S(2)}) copy-start(bf16[4,1,2,128]{3,2,1,0:T(2,128)(2,1)} %nk_ref.1) | copy-start | bytes 6148
  84.0 14.4 %copy-start.3 = (bf16[4,1,2,128]{3,2,1,0:T(2,128)(2,1)S(1)}, bf16[4,1,2,128]{3,2,1,0:T(2,128)(2,1)}, u32[]{:S(2)}) copy-start(bf16[4,1,2,128]{3,2,1,0:T(2,128)(2,1)} %nv_ref.1) | copy-start | bytes 6148
  84.0 45.7 %all-to-all-start.1 = ((f16[16,17,2,128]{3,2,1,0:T(2,128)(2,1)}), f16[16,17,2,128]{3,2,1,0:T(2,128)(2,1)S(1)}, u32[]{:S(2)}, u32[]{:S(2)}) async-start(f16[16,17,2,128]{3,2,1,0:T(2,128)(2,1)} %bitcast.2), calls=%async_computation.1 | async-start | bytes 278528 | tf_op jit(solution)/shard_map/all_to_all | solution.py:284

commit v4 on v3

--- a/solution.py
+++ b/solution.py
@@ -42,13 +42,15 @@
 
 
 def prepare(
-    heads, picks_ref, slots_ref, q_hbm, k_ref, v_ref, ck_ref, cv_ref, pages_ref, ask_ref,
-    q_ref, ck_own, cv_own, arrived,
+    heads, picks_hbm, slots_hbm, q_hbm, k_ref, v_ref, ck_ref, cv_ref, pages_ref, ask_ref,
+    picks_ref, slots_ref, q_ref, ck_own, cv_own, arrived,
 ):
     core = lax.axis_index("row")
     span, width = k_ref.shape[1:]
     near = ck_ref.shape[1]
     moves = (
+        (picks_hbm, picks_ref),
+        (slots_hbm, slots_ref),
         (q_hbm, q_ref),
         (ck_ref.at[core], ck_own),
         (cv_ref.at[core], cv_own),
@@ -61,6 +63,8 @@
     lane = lax.broadcasted_iota(jnp.int32, (8, width), 1)
     sub = lax.broadcasted_iota(jnp.int32, (8, width), 0)
     masks = []
+    for copy in copies[:2]:
+        copy.wait()
     for head in range(heads):
         slot_free = jnp.ones((8, width), jnp.float32)
         cluster_used = jnp.zeros((8, width), jnp.float32)
@@ -69,14 +73,14 @@
             slot_free = jnp.where(lane == slots_ref[head, pick], 0.0, slot_free)
             cluster_used = jnp.where(lane == pick, 1.0, cluster_used)
         masks.append(jnp.where(sub == 0, slot_free, jnp.where(sub == 1, cluster_used, 0.0)))
-    copies[0].wait()
+    copies[2].wait()
     for head in range(heads):
         message = jnp.concatenate(head_queries(q_ref, heads, head) + [masks[head]], axis=0)
         height = message.shape[0] - 8 + EXTRA
         message = message[0:height].astype(ask_ref.dtype)
         for peer in range(head, ask_ref.shape[0] // height, heads):
             ask_ref[peer * height : (peer + 1) * height, :] = message
-    for copy in copies[1:3]:
+    for copy in copies[3:5]:
         copy.wait()
     coarse = jnp.concatenate(
         [ck_own[...].astype(jnp.float32), cv_own[...].astype(jnp.float32)]
@@ -84,7 +88,7 @@
         axis=0,
     )
     pages_ref[2 * span :, :] = coarse.astype(pages_ref.dtype)
-    for copy in copies[3:]:
+    for copy in copies[5:]:
         copy.wait()
 
 
@@ -262,7 +266,6 @@
 
 
 VMEM = pl.BlockSpec(memory_space=pltpu.VMEM)
-SMEM = pl.BlockSpec(memory_space=pltpu.SMEM)
 HBM = pl.BlockSpec(memory_space=pltpu.HBM)
 
 
@@ -299,12 +302,13 @@
             shape((2 * span + 16, width), jnp.bfloat16),
             shape((peers * height, width), jnp.bfloat16),
         ),
-        [SMEM] * 2 + [HBM] * 5,
+        [HBM] * 7,
         2**16,
         60,
-        [pltpu.VMEM(queries.shape, jnp.bfloat16)]
+        [pltpu.SMEM(picks.shape, jnp.int32), pltpu.SMEM(slots.shape, jnp.int32)]
+        + [pltpu.VMEM(queries.shape, jnp.bfloat16)]
         + [pltpu.VMEM((near, width), jnp.bfloat16)] * 2
-        + [pltpu.SemaphoreType.DMA((5,))],
+        + [pltpu.SemaphoreType.DMA((7,))],
     )(picks, slots, queries, keys, values, cent_keys, cent_values)
     every = [(z, c) for z in range(ring) for c in range(cores)]
     shift = lambda of: [(((z + of(c)) % ring) * cores + c, z * cores + c) for z, c in every]

time: 131 us -> 131 us (level)
  no operation moved by 1% of the time
where the time goes in v4:
time: 131 us; the launch traced here: 130 us
  starting transfers between devices  71.7 us (55%)
  waiting for transfers between devices  51.3 us (39%)
  Pallas kernels  6.49 us (5%)
    all_to_all x2, starting transfers between devices, exchange(): lax.all_to_all(pairs, PEERS, 0, 0, tiled=True).reshape(messages.shape)  59.4 us
    all_to_all x2, waiting for transfers between devices, exchange(): lax.all_to_all(pairs, PEERS, 0, 0, tiled=True).reshape(messages.shape)  34.4 us
    ppermute x3, waiting for transfers between devices, per_device(): fetched.append(lax.ppermute(pages, RING + ('row',), pairs))  16.9 us
    ppermute x3, starting transfers between devices, per_device(): fetched.append(lax.ppermute(pages, RING + ('row',), pairs))  12.4 us
    pallas_call x1, Pallas kernels, per_device(): on_core(functools.partial(attend, span, near, peers), shape((peers * heig...  2.94 us
  transfers between devices with their start and end apart: 5, of which 5 were waited for; matrix products, arithmetic and copies ran while one was open for 0% of the time, Pallas kernels for 0%

profile of v4, /device:TPU:33, one launch (start us, length us, event | category | flops | bytes accessed | tf_op | source)
XLA Modules:
  0.0 130.4 jit_solution(15587241123864298956)
XLA Ops:
  0.0 1.8 %shard_map.91 = (bf16[1040,128]{1,0:T(8,128)(2,1)}, bf16[544,128]{1,0:T(8,128)(2,1)}) custom-call(s32[1,2,16]{2,1,0:T(2,128)} %picks_hbm.1, s32[2,128]{1,0:T(2,128)} %slots_hbm.1, bf16[4,1,16,128]{3,2,1,0:T(8,128)(2,1)} %q_ref.1, bf16[2,512,128]{2,1,0:T(8,128)(2,1)} %k_ref.1, bf16[2,512,128]{2,1,0:T(8,128)(2,1)} %v_ref.1, bf16[2,4,128]{2,1,0:T(4,128)(2,1)} %ck_ref.1, ...), custom_call_target="tpu_custom_call" | custom-call | flops 65536 | bytes 1048576 | tf_op jit(solution)/shard_map/pallas_call | solution.py:299
  1.8 0.0 copy-start
  1.9 45.0 %all-to-all-start = ((bf16[16,17,2,128]{3,2,1,0:T(2,128)(2,1)}), bf16[16,17,2,128]{3,2,1,0:T(2,128)(2,1)S(1)}, u32[]{:S(2)}, u32[]{:S(2)}) async-start(bf16[16,17,2,128]{3,2,1,0:T(2,128)(2,1)} %bitcast.7), calls=%async_computation | async-start | bytes 278528 | tf_op jit(solution)/shard_map/all_to_all | solution.py:287
  46.9 0.0 copy-done
  46.9 8.4 %collective-permute-start = (bf16[1040,128]{1,0:T(8,128)(2,1)S(1)}, bf16[1040,128]{1,0:T(8,128)(2,1)S(1)}, u32[]{:S(2)}, u32[]{:S(2)}) collective-permute-start(bf16[1040,128]{1,0:T(8,128)(2,1)S(1)} %copy-done), channel_id=1, source_target_pairs={{8,0},{9,1},{16,8},{17,9},{24,16},{25,17},{32,24},{33,25},{40,32},... | collective-permute-start | bytes 798728 | tf_op jit(solution)/shard_map/ppermute | solution.py:318
  55.3 2.0 %collective-permute-start.1 = (bf16[1040,128]{1,0:T(8,128)(2,1)S(1)}, bf16[1040,128]{1,0:T(8,128)(2,1)S(1)}, u32[]{:S(2)}, u32[]{:S(2)}) collective-permute-start(bf16[1040,128]{1,0:T(8,128)(2,1)S(1)} %copy-done), channel_id=1, source_target_pairs={{248,0},{249,1},{0,8},{1,9},{8,16},{9,17},{16,24},{17,25},{24,32},... | collective-permute-start | bytes 798728 | tf_op jit(solution)/shard_map/ppermute | solution.py:318
  57.3 2.0 %collective-permute-start.2 = (bf16[1040,128]{1,0:T(8,128)(2,1)S(1)}, bf16[1040,128]{1,0:T(8,128)(2,1)S(1)}, u32[]{:S(2)}, u32[]{:S(2)}) collective-permute-start(bf16[1040,128]{1,0:T(8,128)(2,1)S(1)} %copy-done), channel_id=1, source_target_pairs={{16,0},{241,1},{24,8},{249,9},{32,16},{1,17},{40,24},{9,25},{48,32... | collective-permute-start | bytes 798728 | tf_op jit(solution)/shard_map/ppermute | solution.py:318
  59.3 7.7 %collective-permute-done.refs_1_ = bf16[1040,128]{1,0:T(8,128)(2,1)S(1)} collective-permute-done((bf16[1040,128]{1,0:T(8,128)(2,1)S(1)}, bf16[1040,128]{1,0:T(8,128)(2,1)S(1)}, u32[]{:S(2)}, u32[]{:S(2)}) %collective-permute-start) | collective-permute-done | bytes 266272 | tf_op jit(solution)/shard_map/ppermute | solution.py:318
  66.9 3.7 %collective-permute-done.1.refs_2_ = bf16[1040,128]{1,0:T(8,128)(2,1)S(1)} collective-permute-done((bf16[1040,128]{1,0:T(8,128)(2,1)S(1)}, bf16[1040,128]{1,0:T(8,128)(2,1)S(1)}, u32[]{:S(2)}, u32[]{:S(2)}) %collective-permute-start.1) | collective-permute-done | bytes 266272 | tf_op jit(solution)/shard_map/ppermute | solution.py:318
  70.7 5.5 %collective-permute-done.2.refs_3_ = bf16[1040,128]{1,0:T(8,128)(2,1)S(1)} collective-permute-done((bf16[1040,128]{1,0:T(8,128)(2,1)S(1)}, bf16[1040,128]{1,0:T(8,128)(2,1)S(1)}, u32[]{:S(2)}, u32[]{:S(2)}) %collective-permute-start.2) | collective-permute-done | bytes 266272 | tf_op jit(solution)/shard_map/ppermute | solution.py:318
  76.2 0.3 shard_map.92
  76.5 3.2 %all-to-all-done = bf16[16,17,2,128]{3,2,1,0:T(2,128)(2,1)S(1)} async-done(((bf16[16,17,2,128]{3,2,1,0:T(2,128)(2,1)}), bf16[16,17,2,128]{3,2,1,0:T(2,128)(2,1)S(1)}, u32[]{:S(2)}, u32[]{:S(2)}) %all-to-all-start) | async-done | bytes 139296 | tf_op jit(solution)/shard_map/all_to_all | solution.py:287
  79.7 2.9 %shard_map.93 = f32[544,128]{1,0:T(8,128)S(1)} custom-call(bf16[544,128]{1,0:T(8,128)(2,1)S(1)} %bitcast.5, bf16[4,512,256]{2,1,0:T(8,128)(2,1)S(1)} %get-tuple-element.15.keys_ref, bf16[4,128,512]{2,1,0:T(8,128)(2,1)S(1)} %get-tuple-element.16.values_ref, bf16[16,256]{1,0:T(8,128)(2,1)S(1)} %get-tuple-element.17.ends_ref, ...), custom_call_target="tpu_custom_call" | custom-call | flops 536870912 | bytes 1048576 | tf_op jit(solution)/shard_map/pallas_call | solution.py:339
  82.6 0.7 convert_element_type.8
  83.3 0.0 copy-start.1
  83.3 0.0 copy-start.2
  83.3 0.0 copy-start.3
  83.3 14.4 %all-to-all-start.1 = ((f16[16,17,2,128]{3,2,1,0:T(2,128)(2,1)}), f16[16,17,2,128]{3,2,1,0:T(2,128)(2,1)S(1)}, u32[]{:S(2)}, u32[]{:S(2)}) async-start(f16[16,17,2,128]{3,2,1,0:T(2,128)(2,1)} %bitcast.2), calls=%async_computation.1 | async-start | bytes 278528 | tf_op jit(solution)/shard_map/all_to_all | solution.py:287
  97.7 0.0 copy-done.1
  97.7 0.0 copy-done.2
  97.7 0.0 copy-done.3
  97.7 0.1 shard_map.94
  97.8 31.2 %all-to-all-done.1 = f16[16,17,2,128]{3,2,1,0:T(2,128)(2,1)S(1)} async-done(((f16[16,17,2,128]{3,2,1,0:T(2,128)(2,1)}), f16[16,17,2,128]{3,2,1,0:T(2,128)(2,1)S(1)}, u32[]{:S(2)}, u32[]{:S(2)}) %all-to-all-start.1) | async-done | bytes 139296 | tf_op jit(solution)/shard_map/all_to_all | solution.py:287
  129.1 1.3 shard_map.95
  (1 shorter events, 0.0 us)
Async XLA Ops:
  1.8 45.0 %copy-start = (bf16[1040,128]{1,0:T(8,128)(2,1)S(1)}, bf16[1040,128]{1,0:T(8,128)(2,1)}, u32[]{:S(2)}) copy-start(bf16[1040,128]{1,0:T(8,128)(2,1)} %get-tuple-element.14.refs_0_) | copy-start | bytes 798724
  1.9 77.8 %all-to-all-start = ((bf16[16,17,2,128]{3,2,1,0:T(2,128)(2,1)}), bf16[16,17,2,128]{3,2,1,0:T(2,128)(2,1)S(1)}, u32[]{:S(2)}, u32[]{:S(2)}) async-start(bf16[16,17,2,128]{3,2,1,0:T(2,128)(2,1)} %bitcast.7), calls=%async_computation | async-start | bytes 278528 | tf_op jit(solution)/shard_map/all_to_all | solution.py:287
  46.9 20.0 %collective-permute-start = (bf16[1040,128]{1,0:T(8,128)(2,1)S(1)}, bf16[1040,128]{1,0:T(8,128)(2,1)S(1)}, u32[]{:S(2)}, u32[]{:S(2)}) collective-permute-start(bf16[1040,128]{1,0:T(8,128)(2,1)S(1)} %copy-done), channel_id=1, source_target_pairs={{8,0},{9,1},{16,8},{17,9},{24,16},{25,17},{32,24},{33,25},{40,32},... | collective-permute-start | bytes 798728 | tf_op jit(solution)/shard_map/ppermute | solution.py:318
  55.3 15.3 %collective-permute-start.1 = (bf16[1040,128]{1,0:T(8,128)(2,1)S(1)}, bf16[1040,128]{1,0:T(8,128)(2,1)S(1)}, u32[]{:S(2)}, u32[]{:S(2)}) collective-permute-start(bf16[1040,128]{1,0:T(8,128)(2,1)S(1)} %copy-done), channel_id=1, source_target_pairs={{248,0},{249,1},{0,8},{1,9},{8,16},{9,17},{16,24},{17,25},{24,32},... | collective-permute-start | bytes 798728 | tf_op jit(solution)/shard_map/ppermute | solution.py:318
  57.3 18.9 %collective-permute-start.2 = (bf16[1040,128]{1,0:T(8,128)(2,1)S(1)}, bf16[1040,128]{1,0:T(8,128)(2,1)S(1)}, u32[]{:S(2)}, u32[]{:S(2)}) collective-permute-start(bf16[1040,128]{1,0:T(8,128)(2,1)S(1)} %copy-done), channel_id=1, source_target_pairs={{16,0},{241,1},{24,8},{249,9},{32,16},{1,17},{40,24},{9,25},{48,32... | collective-permute-start | bytes 798728 | tf_op jit(solution)/shard_map/ppermute | solution.py:318
  83.3 14.4 %copy-start.1 = (bf16[4,1,16,128]{3,2,1,0:T(8,128)(2,1)S(1)}, bf16[4,1,16,128]{3,2,1,0:T(8,128)(2,1)}, u32[]{:S(2)}) copy-start(bf16[4,1,16,128]{3,2,1,0:T(8,128)(2,1)} %q_ref.1) | copy-start | bytes 49156
  83.3 14.4 %copy-start.2 = (bf16[4,1,2,128]{3,2,1,0:T(2,128)(2,1)S(1)}, bf16[4,1,2,128]{3,2,1,0:T(2,128)(2,1)}, u32[]{:S(2)}) copy-start(bf16[4,1,2,128]{3,2,1,0:T(2,128)(2,1)} %nk_ref.1) | copy-start | bytes 6148
  83.3 14.4 %copy-start.3 = (bf16[4,1,2,128]{3,2,1,0:T(2,128)(2,1)S(1)}, bf16[4,1,2,128]{3,2,1,0:T(2,128)(2,1)}, u32[]{:S(2)}) copy-start(bf16[4,1,2,128]{3,2,1,0:T(2,128)(2,1)} %nv_ref.1) | copy-start | bytes 6148
  83.3 45.7 %all-to-all-start.1 = ((f16[16,17,2,128]{3,2,1,0:T(2,128)(2,1)}), f16[16,17,2,128]{3,2,1,0:T(2,128)(2,1)S(1)}, u32[]{:S(2)}, u32[]{:S(2)}) async-start(f16[16,17,2,128]{3,2,1,0:T(2,128)(2,1)} %bitcast.2), calls=%async_computation.1 | async-start | bytes 278528 | tf_op jit(solution)/shard_map/all_to_all | solution.py:287

commit v5 on v4

--- a/solution.py
+++ b/solution.py
@@ -31,7 +31,7 @@
 
 
 def near_offsets(core):
-    return (0, 1, -1, 2 - 4 * core)
+    return (0, 1 - 2 * core, 2 * core - 1, 2 - 4 * core)
 
 
 def head_queries(q_ref, heads, head):
@@ -42,21 +42,24 @@
 
 
 def prepare(
-    heads, picks_hbm, slots_hbm, q_hbm, k_ref, v_ref, ck_ref, cv_ref, pages_ref, ask_ref,
-    picks_ref, slots_ref, q_ref, ck_own, cv_own, arrived,
+    heads, picks_hbm, slots_hbm, q_hbm, k_ref, v_ref, ck_ref, cv_ref, own_ref, both_ref, ask_ref,
+    picks_ref, slots_ref, q_ref, ck_all, cv_all, arrived,
 ):
     core = lax.axis_index("row")
     span, width = k_ref.shape[1:]
     near = ck_ref.shape[1]
-    moves = (
+    size = own_ref.shape[0]
+    places = ((core, own_ref, 0), (core, both_ref, 0), (1 - core, both_ref, size))
+    moves = [
         (picks_hbm, picks_ref),
         (slots_hbm, slots_ref),
         (q_hbm, q_ref),
-        (ck_ref.at[core], ck_own),
-        (cv_ref.at[core], cv_own),
-        (k_ref.at[core], pages_ref.at[pl.ds(0, span)]),
-        (v_ref.at[core], pages_ref.at[pl.ds(span, span)]),
-    )
+        (ck_ref, ck_all),
+        (cv_ref, cv_all),
+    ]
+    for head, target, at in places:
+        moves.append((k_ref.at[head], target.at[pl.ds(at, span)]))
+        moves.append((v_ref.at[head], target.at[pl.ds(at + span, span)]))
     copies = [pltpu.make_async_copy(*move, arrived.at[i]) for i, move in enumerate(moves)]
     for copy in copies:
         copy.start()
@@ -82,12 +85,13 @@
             ask_ref[peer * height : (peer + 1) * height, :] = message
     for copy in copies[3:5]:
         copy.wait()
-    coarse = jnp.concatenate(
-        [ck_own[...].astype(jnp.float32), cv_own[...].astype(jnp.float32)]
-        + [jnp.zeros((16 - 2 * near, width), jnp.float32)],
-        axis=0,
-    )
-    pages_ref[2 * span :, :] = coarse.astype(pages_ref.dtype)
+    for head, target, at in places:
+        coarse = jnp.concatenate(
+            [ck_all[head].astype(jnp.float32), cv_all[head].astype(jnp.float32)]
+            + [jnp.zeros((16 - 2 * near, width), jnp.float32)],
+            axis=0,
+        )
+        target[at + 2 * span : at + size, :] = coarse.astype(target.dtype)
     for copy in copies[5:]:
         copy.wait()
 
@@ -120,7 +124,8 @@
 
 def arrange(span, near, ring, *refs):
     page_refs, (keys_ref, values_ref, ends_ref, end_values_ref) = refs[:NEAR], refs[NEAR:]
-    width = page_refs[0].shape[1]
+    size, width = page_refs[0].shape
+    starts = (0, 0, size, 0)
     position, core = place()
     shards = [lax.rem(position + off + ring, ring) for off in near_offsets(core)]
     page = span // near
@@ -128,14 +133,17 @@
     row = lax.broadcasted_iota(jnp.int32, (NEAR * near, width), 0)
     column = lax.broadcasted_iota(jnp.int32, (NEAR * near, width), 1)
     cluster = jnp.full((NEAR * near, width), -1, jnp.int32)
-    for b, (ref, shard) in enumerate(zip(page_refs, shards)):
-        keys_ref[b, :, 0:width] = ref[0:span, :]
+    for b, (ref, shard, at) in enumerate(zip(page_refs, shards, starts)):
+        keys_ref[b, :, 0:width] = ref[at : at + span, :]
         for p in range(near):
             picker = jnp.where(lane == shard * near + p, MASKED, 0.0)
             keys_ref[b, p * page : (p + 1) * page, width:] = picker.astype(jnp.bfloat16)
-        values_ref[b] = jnp.transpose(ref[span : 2 * span, :])
+        values_ref[b] = jnp.transpose(ref[at + span : at + 2 * span, :])
         cluster = jnp.where(row // near == b, shard * near + row - b * near, cluster)
-    ends = [ref[2 * span :, :].astype(jnp.float32) for ref in page_refs]
+    ends = [
+        ref[at + 2 * span : at + size, :].astype(jnp.float32)
+        for ref, at in zip(page_refs, starts)
+    ]
     picker = jnp.where(column == cluster, MASKED, 0.0)
     coarse = jnp.concatenate([e[0:near] for e in ends], axis=0)
     ends_ref[...] = jnp.concatenate([coarse, picker], axis=1).astype(jnp.bfloat16)
@@ -296,10 +304,12 @@
     per_peer = num_steps * num_heads // heads
     height = per_peer + EXTRA
     shape = jax.ShapeDtypeStruct
-    pages, ask = on_core(
+    size = 2 * span + 16
+    own, both, ask = on_core(
         functools.partial(prepare, heads),
         (
-            shape((2 * span + 16, width), jnp.bfloat16),
+            shape((size, width), jnp.bfloat16),
+            shape((2 * size, width), jnp.bfloat16),
             shape((peers * height, width), jnp.bfloat16),
         ),
         [HBM] * 7,
@@ -307,15 +317,21 @@
         60,
         [pltpu.SMEM(picks.shape, jnp.int32), pltpu.SMEM(slots.shape, jnp.int32)]
         + [pltpu.VMEM(queries.shape, jnp.bfloat16)]
-        + [pltpu.VMEM((near, width), jnp.bfloat16)] * 2
-        + [pltpu.SemaphoreType.DMA((7,))],
+        + [pltpu.VMEM((heads, near, width), jnp.bfloat16)] * 2
+        + [pltpu.SemaphoreType.DMA((11,))],
     )(picks, slots, queries, keys, values, cent_keys, cent_values)
     every = [(z, c) for z in range(ring) for c in range(cores)]
-    shift = lambda of: [(((z + of(c)) % ring) * cores + c, z * cores + c) for z, c in every]
-    fetched = [pages]
-    for i in range(1, NEAR):
-        pairs = shift(lambda c: near_offsets(c)[i])
-        fetched.append(lax.ppermute(pages, RING + ("row",), pairs))
+
+    def from_offset(pages, i):
+        pairs = [
+            (((z + near_offsets(c)[i]) % ring) * cores + c, z * cores + c) for z, c in every
+        ]
+        return lax.ppermute(pages, RING + ("row",), pairs)
+
+    beside = from_offset(both, 1)
+    beyond = from_offset(own, 3)
+    swapped = lax.ppermute(beside, "row", [(0, 1), (1, 0)])
+    fetched = (own, beside, swapped, beyond)
     asked = exchange(ask, peers)
     tail_out, tail_stat = on_core(
         functools.partial(tail, heads),

time: 131 us -> 129 us (0.985)
  waiting for transfers between devices: 51.3 us -> 48.7 us
    ppermute x3, starting transfers between devices: 12.4 us -> 20.5 us  [the longest x1 13.1 us: per_device(): swapped = lax.ppermute(beside, 'row', [(0, 1), (1, 0)])]
    all_to_all x2, starting transfers between devices: 59.4 us -> 51.7 us  [exchange(): lax.all_to_all(pairs, PEERS, 0, 0, tiled=True).reshape(messages.shape)]
    ppermute x3, waiting for transfers between devices: 16.9 us -> 13.9 us  [the longest x2 13.9 us: from_offset(): return lax.ppermute(pages, RING + ('row',), pairs)]
  transfers between devices with their start and end apart: 5 -> 5, of which waited for: 5 -> 4; matrix products, arithmetic and copies ran while one was open for 0% -> 0% of each run, Pallas kernels for 0% -> 0%
where the time goes in v5:
time: 129 us
  starting transfers between devices  72.2 us (56%)
  waiting for transfers between devices  48.7 us (38%)
  Pallas kernels  6.92 us (5%)
    all_to_all x2, starting transfers between devices, exchange(): lax.all_to_all(pairs, PEERS, 0, 0, tiled=True).reshape(messages.shape)  51.7 us
    all_to_all x2, waiting for transfers between devices, exchange(): lax.all_to_all(pairs, PEERS, 0, 0, tiled=True).reshape(messages.shape)  34.8 us
    ppermute x2, waiting for transfers between devices, from_offset(): return lax.ppermute(pages, RING + ('row',), pairs)  13.9 us
    ppermute x1, starting transfers between devices, per_device(): swapped = lax.ppermute(beside, 'row', [(0, 1), (1, 0)])  13.1 us
    ppermute x2, starting transfers between devices, from_offset(): return lax.ppermute(pages, RING + ('row',), pairs)  7.34 us
    pallas_call x1, Pallas kernels, per_device(): on_core(functools.partial(attend, span, near, peers), shape((peers * heig...  2.94 us
  transfers between devices with their start and end apart: 5, of which 4 were waited for; matrix products, arithmetic and copies ran while one was open for 0% of the time, Pallas kernels for 0%

profile of v5, /device:TPU:33, one launch (start us, length us, event | category | flops | bytes accessed | tf_op | source)
XLA Modules:
  0.0 128.7 jit_solution(2417731341941704295)
XLA Ops:
  0.0 2.3 %shard_map.91 = (bf16[1040,128]{1,0:T(8,128)(2,1)}, bf16[2080,128]{1,0:T(8,128)(2,1)}, bf16[544,128]{1,0:T(8,128)(2,1)}) custom-call(s32[1,2,16]{2,1,0:T(2,128)} %picks_hbm.1, s32[2,128]{1,0:T(2,128)} %slots_hbm.1, bf16[4,1,16,128]{3,2,1,0:T(8,128)(2,1)} %q_ref.1, bf16[2,512,128]{2,1,0:T(8,128)(2,1)} %k_ref.1, bf16[2,512,128]{2,1,0:T(8,128)(2,1)} %v_ref.1, ...), custom_call_target="tpu_custom_call" | custom-call | flops 65536 | bytes 1048576 | tf_op jit(solution)/shard_map/pallas_call | solution.py:308
  2.3 0.0 copy-start
  2.3 5.4 %collective-permute-start = (bf16[2080,128]{1,0:T(8,128)(2,1)}, bf16[2080,128]{1,0:T(8,128)(2,1)S(1)}, u32[]{:S(2)}, u32[]{:S(2)}) collective-permute-start(bf16[2080,128]{1,0:T(8,128)(2,1)} %get-tuple-element.16), channel_id=1, source_target_pairs={{8,0},{249,1},{16,8},{1,9},{24,16},{9,17},{32,24},{17,25},{40,32},... | collective-permute-start | bytes 1597448 | tf_op jit(solution)/shard_map/ppermute | solution.py:329
  7.7 44.8 %all-to-all-start = ((bf16[16,17,2,128]{3,2,1,0:T(2,128)(2,1)}), bf16[16,17,2,128]{3,2,1,0:T(2,128)(2,1)S(1)}, u32[]{:S(2)}, u32[]{:S(2)}) async-start(bf16[16,17,2,128]{3,2,1,0:T(2,128)(2,1)} %bitcast.7), calls=%async_computation | async-start | bytes 278528 | tf_op jit(solution)/shard_map/all_to_all | solution.py:295
  52.5 2.6 %collective-permute-done.refs_1_ = bf16[2080,128]{1,0:T(8,128)(2,1)S(1)} collective-permute-done((bf16[2080,128]{1,0:T(8,128)(2,1)}, bf16[2080,128]{1,0:T(8,128)(2,1)S(1)}, u32[]{:S(2)}, u32[]{:S(2)}) %collective-permute-start) | collective-permute-done | bytes 532512 | tf_op jit(solution)/shard_map/ppermute | solution.py:329
  55.2 13.1 %collective-permute-start.1 = (bf16[2080,128]{1,0:T(8,128)(2,1)S(1)}, bf16[2080,128]{1,0:T(8,128)(2,1)S(1)}, u32[]{:S(2)}, u32[]{:S(2)}) collective-permute-start(bf16[2080,128]{1,0:T(8,128)(2,1)S(1)} %collective-permute-done.refs_1_), channel_id=1, source_target_pairs={{0,1},{1,0},{2,3},{3,2},{4,5},{5,4},{6,7},{7,6},{8,9},{9,8},{10,11... | collective-permute-start | bytes 1597448 | tf_op jit(solution)/shard_map/ppermute | solution.py:333
  68.3 0.0 copy-done
  68.3 2.0 %collective-permute-start.2 = (bf16[1040,128]{1,0:T(8,128)(2,1)S(1)}, bf16[1040,128]{1,0:T(8,128)(2,1)S(1)}, u32[]{:S(2)}, u32[]{:S(2)}) collective-permute-start(bf16[1040,128]{1,0:T(8,128)(2,1)S(1)} %copy-done), channel_id=1, source_target_pairs={{16,0},{241,1},{24,8},{249,9},{32,16},{1,17},{40,24},{9,25},{48,32... | collective-permute-start | bytes 798728 | tf_op jit(solution)/shard_map/ppermute | solution.py:329
  70.3 11.2 %collective-permute-done.2.refs_3_ = bf16[1040,128]{1,0:T(8,128)(2,1)S(1)} collective-permute-done((bf16[1040,128]{1,0:T(8,128)(2,1)S(1)}, bf16[1040,128]{1,0:T(8,128)(2,1)S(1)}, u32[]{:S(2)}, u32[]{:S(2)}) %collective-permute-start.2) | collective-permute-done | bytes 266272 | tf_op jit(solution)/shard_map/ppermute | solution.py:329
  81.5 0.0 collective-permute-done.1.refs_2_
  81.5 0.3 shard_map.92
  81.8 4.4 %all-to-all-done = bf16[16,17,2,128]{3,2,1,0:T(2,128)(2,1)S(1)} async-done(((bf16[16,17,2,128]{3,2,1,0:T(2,128)(2,1)}), bf16[16,17,2,128]{3,2,1,0:T(2,128)(2,1)S(1)}, u32[]{:S(2)}, u32[]{:S(2)}) %all-to-all-start) | async-done | bytes 139296 | tf_op jit(solution)/shard_map/all_to_all | solution.py:295
  86.2 2.9 %shard_map.93 = f32[544,128]{1,0:T(8,128)S(1)} custom-call(bf16[544,128]{1,0:T(8,128)(2,1)S(1)} %bitcast.5, bf16[4,512,256]{2,1,0:T(8,128)(2,1)S(1)} %get-tuple-element.17.keys_ref, bf16[4,128,512]{2,1,0:T(8,128)(2,1)S(1)} %get-tuple-element.18.values_ref, bf16[16,256]{1,0:T(8,128)(2,1)S(1)} %get-tuple-element.19.ends_ref, ...), custom_call_target="tpu_custom_call" | custom-call | flops 536870912 | bytes 1048576 | tf_op jit(solution)/shard_map/pallas_call | solution.py:355
  89.2 0.7 convert_element_type.8
  89.8 0.0 copy-start.1
  89.8 0.0 copy-start.2
  89.8 0.0 copy-start.3
  89.8 6.9 %all-to-all-start.1 = ((f16[16,17,2,128]{3,2,1,0:T(2,128)(2,1)}), f16[16,17,2,128]{3,2,1,0:T(2,128)(2,1)S(1)}, u32[]{:S(2)}, u32[]{:S(2)}) async-start(f16[16,17,2,128]{3,2,1,0:T(2,128)(2,1)} %bitcast.2), calls=%async_computation.1 | async-start | bytes 278528 | tf_op jit(solution)/shard_map/all_to_all | solution.py:295
  96.8 0.0 copy-done.1
  96.8 0.0 copy-done.2
  96.8 0.0 copy-done.3
  96.8 0.1 shard_map.94
  96.9 30.4 %all-to-all-done.1 = f16[16,17,2,128]{3,2,1,0:T(2,128)(2,1)S(1)} async-done(((f16[16,17,2,128]{3,2,1,0:T(2,128)(2,1)}), f16[16,17,2,128]{3,2,1,0:T(2,128)(2,1)S(1)}, u32[]{:S(2)}, u32[]{:S(2)}) %all-to-all-start.1) | async-done | bytes 139296 | tf_op jit(solution)/shard_map/all_to_all | solution.py:295
  127.4 1.3 %shard_map.95 = bf16[4,1,16,128]{3,2,1,0:T(8,128)(2,1)} custom-call(f32[544,128]{1,0:T(8,128)S(1)} %convert.1.reply_ref, f32[2,32,128]{2,1,0:T(8,128)S(1)} %get-tuple-element.21.tail_ref, f32[2,32,128]{2,1,0:T(8,128)S(1)} %get-tuple-element.22.tail_stat_ref), custom_call_target="tpu_custom_call" | custom-call | flops 1048576 | bytes 1048576 | tf_op jit(solution)/shard_map/pallas_call | solution.py:363
  (1 shorter events, 0.0 us)
Async XLA Ops:
  2.3 66.0 %copy-start = (bf16[1040,128]{1,0:T(8,128)(2,1)S(1)}, bf16[1040,128]{1,0:T(8,128)(2,1)}, u32[]{:S(2)}) copy-start(bf16[1040,128]{1,0:T(8,128)(2,1)} %get-tuple-element.15.refs_0_) | copy-start | bytes 798724
  2.3 52.9 %collective-permute-start = (bf16[2080,128]{1,0:T(8,128)(2,1)}, bf16[2080,128]{1,0:T(8,128)(2,1)S(1)}, u32[]{:S(2)}, u32[]{:S(2)}) collective-permute-start(bf16[2080,128]{1,0:T(8,128)(2,1)} %get-tuple-element.16), channel_id=1, source_target_pairs={{8,0},{249,1},{16,8},{1,9},{24,16},{9,17},{32,24},{17,25},{40,32},... | collective-permute-start | bytes 1597448 | tf_op jit(solution)/shard_map/ppermute | solution.py:329
  7.7 78.5 %all-to-all-start = ((bf16[16,17,2,128]{3,2,1,0:T(2,128)(2,1)}), bf16[16,17,2,128]{3,2,1,0:T(2,128)(2,1)S(1)}, u32[]{:S(2)}, u32[]{:S(2)}) async-start(bf16[16,17,2,128]{3,2,1,0:T(2,128)(2,1)} %bitcast.7), calls=%async_computation | async-start | bytes 278528 | tf_op jit(solution)/shard_map/all_to_all | solution.py:295
  55.2 26.4 %collective-permute-start.1 = (bf16[2080,128]{1,0:T(8,128)(2,1)S(1)}, bf16[2080,128]{1,0:T(8,128)(2,1)S(1)}, u32[]{:S(2)}, u32[]{:S(2)}) collective-permute-start(bf16[2080,128]{1,0:T(8,128)(2,1)S(1)} %collective-permute-done.refs_1_), channel_id=1, source_target_pairs={{0,1},{1,0},{2,3},{3,2},{4,5},{5,4},{6,7},{7,6},{8,9},{9,8},{10,11... | collective-permute-start | bytes 1597448 | tf_op jit(solution)/shard_map/ppermute | solution.py:333
  68.3 13.2 %collective-permute-start.2 = (bf16[1040,128]{1,0:T(8,128)(2,1)S(1)}, bf16[1040,128]{1,0:T(8,128)(2,1)S(1)}, u32[]{:S(2)}, u32[]{:S(2)}) collective-permute-start(bf16[1040,128]{1,0:T(8,128)(2,1)S(1)} %copy-done), channel_id=1, source_target_pairs={{16,0},{241,1},{24,8},{249,9},{32,16},{1,17},{40,24},{9,25},{48,32... | collective-permute-start | bytes 798728 | tf_op jit(solution)/shard_map/ppermute | solution.py:329
  89.8 6.9 %copy-start.1 = (bf16[4,1,16,128]{3,2,1,0:T(8,128)(2,1)S(1)}, bf16[4,1,16,128]{3,2,1,0:T(8,128)(2,1)}, u32[]{:S(2)}) copy-start(bf16[4,1,16,128]{3,2,1,0:T(8,128)(2,1)} %q_ref.1) | copy-start | bytes 49156
  89.8 6.9 %copy-start.2 = (bf16[4,1,2,128]{3,2,1,0:T(2,128)(2,1)S(1)}, bf16[4,1,2,128]{3,2,1,0:T(2,128)(2,1)}, u32[]{:S(2)}) copy-start(bf16[4,1,2,128]{3,2,1,0:T(2,128)(2,1)} %nk_ref.1) | copy-start | bytes 6148
  89.8 6.9 %copy-start.3 = (bf16[4,1,2,128]{3,2,1,0:T(2,128)(2,1)S(1)}, bf16[4,1,2,128]{3,2,1,0:T(2,128)(2,1)}, u32[]{:S(2)}) copy-start(bf16[4,1,2,128]{3,2,1,0:T(2,128)(2,1)} %nv_ref.1) | copy-start | bytes 6148
  89.8 37.5 %all-to-all-start.1 = ((f16[16,17,2,128]{3,2,1,0:T(2,128)(2,1)}), f16[16,17,2,128]{3,2,1,0:T(2,128)(2,1)S(1)}, u32[]{:S(2)}, u32[]{:S(2)}) async-start(f16[16,17,2,128]{3,2,1,0:T(2,128)(2,1)} %bitcast.2), calls=%async_computation.1 | async-start | bytes 278528 | tf_op jit(solution)/shard_map/all_to_all | solution.py:295
